TPU v7x, 128 devices: a whole 4x4x4 slice. The times are simulated.
128 devices in a mesh: op: 4 (over z), row: 32 (over y, x, core).
Axes of the slice: x: 4, y: 4, z: 4, core: 2. Of those that a mesh axis runs over, the one named last changes fastest.
Arguments:
- wannier_ops: bfloat16 [2, 4000, 2, 128, 128], P(None, 'row'), may hold values from -0.09375 to 0.09375
- r_coords: int32 [4000, 3], P('row'), may hold values from -8 to 8
- degeneracy: int32 [4000], P('row'), may hold values from 1 to 4
- kpoints: int32 [256, 3], replicated, may hold values from 0 to 15
- bloch_vectors: bfloat16 [256, 2, 64, 128], P(('op', 'row')), may hold values from -0.375 to 0.375
Outputs:
- covariant: float32 [256, 2, 4096], P(('op', 'row'))
Inputs may be any that keep to these rules, and one draw needn't show every extreme that they name: `r_coords`: these coordinates are small integers; a program may pack several of them into one int32 word when it moves them. `degeneracy`: these degeneracies are small integers; a program may pack several of them into one int32 word when it moves them.
All inputs are finite; a program needn't handle non-finite values.
Results may differ from a plain program's by a relative error of at most 0.0038.
Values may be sent and summed in bfloat16 or wider, within the bound.
A program may use at most 192 MiB of HBM per device.

v0:
```python
import math

import jax
import jax.numpy as jnp
from jax import lax
from jax.sharding import PartitionSpec as P

GRID = 16
RMAX = 8


TWO_PI = 6.283185307179586
HIGH = lax.Precision.HIGHEST


def in_one_piece(arrays, axis, dim, along):
    widths = [math.prod(a.shape[along:]) for a in arrays]
    both = jnp.concatenate(
        [a.reshape(*a.shape[:along], w) for a, w in zip(arrays, widths)], axis=along
    )
    whole = lax.all_gather(both, axis, axis=dim, tiled=True)
    parts = jnp.split(whole, [sum(widths[:k]) for k in range(1, len(widths))], axis=along)
    return tuple((b.reshape(*whole.shape[:along], *a.shape[along:]) for a, b in zip(arrays, parts)))


def split_up(x, dim, peers):
    before, after = (x.shape[:dim], x.shape[dim + 1 :])
    return jnp.moveaxis(x.reshape(*before, peers, -1, *after), dim, 0)


def piece_ends(length, count):
    step = length // count
    if step >= 8:
        step -= step % 8
    return [step * k for k in range(1, count)]


def joined_along(parts, dim):
    parts = jnp.moveaxis(parts, 0, dim)
    shape = parts.shape
    return parts.reshape(*shape[:dim], shape[dim] * shape[dim + 1], *shape[dim + 2 :])


def several_exchanges(x, axis, pieces, split_dim, concat_dim):
    parts = split_up(x, split_dim, lax.axis_size(axis))
    widest = max(range(1, max(2, parts.ndim - 1)), key=lambda d: parts.shape[d])
    gathered = []
    for section in jnp.split(parts, piece_ends(parts.shape[widest], pieces), axis=widest):
        if section.size:
            gathered.append(lax.all_to_all(section, axis, split_axis=0, concat_axis=0, tiled=True))
    return joined_along(jnp.concatenate(gathered, axis=widest), concat_dim)


def phase_parts(r_coords, degeneracy, kpoints):
    turns_int = jnp.sum(r_coords[:, None, :] * kpoints[None, :, :], axis=2) % GRID
    angles = turns_int.astype(jnp.float32) * (TWO_PI / GRID)
    weights = 1.0 / degeneracy.astype(jnp.float32)
    cosine = jnp.cos(angles) * weights[:, None]
    sine_part = jnp.sin(angles) * weights[:, None]
    along_x = (r_coords[:, 0].astype(jnp.float32) / RMAX)[:, None]
    return (cosine, sine_part, along_x)


def fourier(phase_re, phase_im, flat_ops):
    stacked = jnp.concatenate([phase_re, phase_im], axis=1)
    product_sum = lax.dot_general(
        stacked, flat_ops, (((0,), (0,)), ((), ())), preferred_element_type=jnp.float32
    )
    k_count = phase_re.shape[1]
    half_cols = flat_ops.shape[1] // 2
    real_part = product_sum[:k_count, :half_cols] - product_sum[k_count:, half_cols:]
    imag_part = product_sum[:k_count, half_cols:] + product_sum[k_count:, :half_cols]
    return (real_part, imag_part)


def complex_mul(form, left, right):

    def single(first, second):
        return jnp.einsum(form, first, second, precision=HIGH)

    return (
        single(left[0], right[0]) - single(left[1], right[1]),
        single(left[0], right[1]) + single(left[1], right[0]),
    )


def rotate(op_pair, vec_pair):
    left_side = complex_mul("knm,kmp->knp", (vec_pair[0], -vec_pair[1]), op_pair)
    return complex_mul("knm,kpm->knp", left_side, vec_pair)


def covariant_form(ham, deriv, posit, posit_deriv):
    band_count = ham[0].shape[-1]
    factor = 1.0 / math.sqrt(band_count)
    form = "kab,kbc->kac"
    a_d = complex_mul(form, posit, deriv)
    d_a = complex_mul(form, deriv, posit)
    h_a = complex_mul(form, ham, posit)
    a_h = complex_mul(form, posit, ham)
    g_real = posit_deriv[0] + factor * (h_a[0] + a_h[0] - (a_d[1] - d_a[1]))
    g_imag = posit_deriv[1] + factor * (h_a[1] + a_h[1] + (a_d[0] - d_a[0]))
    k_count = g_real.shape[0]
    return jnp.stack([g_real.reshape(k_count, -1), g_imag.reshape(k_count, -1)], axis=1)


def make_phases(coords, degens, kpoints, derive):
    cosine, sine_part, along_x = phase_parts(coords, degens, kpoints)
    phase_re = jnp.where(derive, -along_x * sine_part, cosine).astype(jnp.bfloat16)
    phase_im = jnp.where(derive, along_x * cosine, sine_part).astype(jnp.bfloat16)
    return (phase_re, phase_im)


def on_device(wannier_ops, r_coords, degeneracy, kpoints, bloch_vectors):
    row_count = lax.axis_size("row")
    op_count = lax.axis_size("op")
    component = lax.axis_index("op")
    base_ops = lax.dynamic_index_in_dim(wannier_ops, component // 2, 0, keepdims=False)
    r_local = base_ops.shape[0]
    width = base_ops.shape[-1]
    derive = component % 2 == 1
    total_k = kpoints.shape[0]
    per_block = total_k // (row_count * op_count)
    vectors = bloch_vectors.astype(jnp.float32)
    vec_pair = (vectors[:, 0], vectors[:, 1])
    every_coords, every_degen = in_one_piece((r_coords, degeneracy), "row", 0, 1)
    phase_re, phase_im = make_phases(every_coords, every_degen, kpoints, derive)
    entry_ops = base_ops.reshape(r_local, 2, width * width)
    moved = several_exchanges(entry_ops, "row", 2, 2, 0)
    all_r = moved.shape[0]
    slice_cols = moved.shape[2]
    real_part, imag_part = fourier(phase_re, phase_im, moved.reshape(all_r, 2 * slice_cols))
    local_sums = jnp.stack([real_part, imag_part], axis=1)[None]
    owned = lax.all_to_all(local_sums, ("op", "row"), split_axis=1, concat_axis=0, tiled=True)
    owned = owned.reshape(op_count, row_count, per_block, 2, slice_cols)
    owned = jnp.transpose(owned, (0, 2, 3, 1, 4)).reshape(op_count, per_block, 2, width * width)
    rotated = []
    for component_id in range(4):
        op_pair = (
            owned[component_id, :, 0].reshape(per_block, width, width),
            owned[component_id, :, 1].reshape(per_block, width, width),
        )
        rotated.append(rotate(op_pair, vec_pair))
    return covariant_form(rotated[0], rotated[1], rotated[2], rotated[3])


def solution(mesh):
    in_specs = (
        P(None, "row", None, None, None),
        P("row", None),
        P("row"),
        P(),
        P(("op", "row"), None, None, None),
    )
    out_specs = P(("op", "row"), None, None)
    return jax.shard_map(
        on_device, mesh=mesh, in_specs=in_specs, out_specs=out_specs, check_vma=False
    )
```

profile of v0, /device:TPU:1, one launch (start us, length us, event | category | flops | bytes accessed | tf_op | source)
XLA Modules:
  0.0 264.7 jit_solution(8764710877351975365)
XLA Ops:
  0.0 10.1 %constant_dynamic-slice_fusion = bf16[1,125,2,128,128]{4,3,2,1,0:T(8,128)(2,1)} fusion(bf16[2,125,2,128,128]{4,3,2,1,0:T(8,128)(2,1)} %param.5, s32[]{:T(128)S(6)} %select_n.39), kind=kLoop, calls=%fused_computation.119 | loop fusion | bytes 16384004 | tf_op jit(solution)/shard_map/jit(dynamic_index_in_dim)/dynamic_slice | solution.py:117
  10.1 12.5 %copy.44 = bf16[1,125,2,128,128]{1,4,3,2,0:T(8,128)(2,1)} copy(bf16[1,125,2,128,128]{4,3,2,1,0:T(8,128)(2,1)} %constant_dynamic-slice_fusion) | data formatting | bytes 16384000 | tf_op jit(solution)/shard_map/jit(dynamic_index_in_dim)/dynamic_slice | solution.py:117
  22.7 8.4 %copy.45 = bf16[32,56,2,512]{3,1,2,0:T(8,128)(2,1)} copy(bf16[32,56,2,512]{1,3,0,2:T(8,128)(2,1)} %bitcast.204) | data formatting | bytes 7340032 | tf_op jit(solution)/shard_map/split | solution.py:48
  31.1 8.6 %all-to-all-start = ((bf16[32,56,2,512]{3,1,2,0:T(8,128)(2,1)}), bf16[32,56,2,512]{3,1,2,0:T(8,128)(2,1)}, u32[]{:S(2)}, u32[]{:S(2)}) async-start(bf16[32,56,2,512]{3,1,2,0:T(8,128)(2,1)} %copy.45), calls=%async_computation | async-start | bytes 7340032 | tf_op jit(solution)/shard_map/all_to_all | solution.py:50
  39.7 9.0 %split.19 = bf16[32,69,2,512]{1,3,0,2:T(8,128)(2,1)} slice(bf16[32,125,2,512]{1,3,0,2:T(8,128)(2,1)} %bitcast.205), slice={[0:32], [56:125], [0:2], [0:512]} | slice | bytes 9043968 | tf_op jit(solution)/shard_map/split | solution.py:48
  48.8 15.1 %copy.46 = bf16[32,69,2,512]{3,2,1,0:T(2,128)(2,1)} copy(bf16[32,69,2,512]{1,3,0,2:T(8,128)(2,1)} %split.19) | data formatting | bytes 9043968 | tf_op jit(solution)/shard_map/split | solution.py:48
  63.9 21.3 %all-to-all-done = bf16[32,56,2,512]{3,1,2,0:T(8,128)(2,1)} async-done(((bf16[32,56,2,512]{3,1,2,0:T(8,128)(2,1)}), bf16[32,56,2,512]{3,1,2,0:T(8,128)(2,1)}, u32[]{:S(2)}, u32[]{:S(2)}) %all-to-all-start) | async-done | bytes 3670048 | tf_op jit(solution)/shard_map/all_to_all | solution.py:50
  85.1 7.3 %all-to-all-start.1 = ((bf16[32,69,2,512]{3,2,1,0:T(2,128)(2,1)}), bf16[32,69,2,512]{3,2,1,0:T(2,128)(2,1)}, u32[]{:S(2)}, u32[]{:S(2)}) async-start(bf16[32,69,2,512]{3,2,1,0:T(2,128)(2,1)} %copy.46), calls=%async_computation.1 | async-start | bytes 9043968 | tf_op jit(solution)/shard_map/all_to_all | solution.py:50
  92.4 71.8 %all-gather = s32[32,125,4]{1,2,0:T(4,128)S(1)} all-gather(s32[1,125,4]{1,2,0:T(4,128)S(1)} %add_bitcast_fusion), channel_id=1, replica_groups=mesh['op'=4,'row'=32] {'row'}, dimensions={0}, use_global_device_ids=true | all-gather | bytes 66000 | tf_op jit(solution)/shard_map/all_gather | solution.py:21
  164.4 5.1 %multiply_reduce_fusion = s32[4000,256]{1,0:T(8,128)S(1)} fusion(s32[256,3]{0,1:T(4,128)S(1)} %copy-done.1, s32[4000,3]{0,1:T(4,128)S(1)} %bitcast.226), kind=kLoop, calls=%fused_computation | loop fusion | flops 5120000 | bytes 4147072 | tf_op jit(solution)/shard_map/reduce_sum | solution.py:55
  169.5 20.3 %select_convert_fusion.1 = (bf16[4000,256]{1,0:T(8,128)(2,1)}, bf16[4000,256]{1,0:T(8,128)(2,1)}) fusion(f32[4000]{0:T(1024)S(1)} %bitcast.228, f32[4000]{0:T(1024)S(1)} %bitcast.227, pred[]{:T(512)S(6)} %eq.7, s32[4000,256]{1,0:T(8,128)S(1)} %multiply_reduce_fusion, f32[4000]{0:T(1024)S(1)} %bitcast.229), kind=kLoop, calls=%fused_computation.13 | loop fusion | flops 21504000 | bytes 8240001 | tf_op jit(solution)/shard_map/convert_element_type | solution.py:108
  189.9 7.5 %copy.47 = bf16[32,56,2,512]{3,2,1,0:T(2,128)(2,1)} copy(bf16[32,56,2,512]{3,1,2,0:T(8,128)(2,1)} %all-to-all-done) | data formatting | bytes 7340032 | tf_op jit(solution)/shard_map/all_to_all | solution.py:50
  197.4 12.2 %pad_maximum_fusion = bf16[32,125,2,512]{3,2,1,0:T(2,128)(2,1)S(1)} fusion(bf16[32,69,2,512]{3,2,1,0:T(2,128)(2,1)} %all-to-all-done.1, bf16[32,56,2,512]{3,2,1,0:T(2,128)(2,1)} %copy.47), kind=kLoop, calls=%fused_computation.1 | loop fusion | flops 4096000 | bytes 16384000 | tf_op jit(solution)/shard_map/concatenate | solution.py:51
  209.6 5.8 %copy.58 = bf16[500,8,2,512]{3,1,2,0:T(8,128)(2,1)} copy(bf16[500,8,2,512]{3,2,1,0:T(2,128)(2,1)S(1)} %bitcast.206) | data formatting | bytes 16384000
  215.3 8.2 %fusion.3 = f32[512,1024]{1,0:T(8,128)S(1)} fusion(bf16[4000,1024]{1,0:T(8,128)(2,1)} %bitcast.207, bf16[4000,256]{1,0:T(8,128)(2,1)} %get-tuple-element.6, bf16[4000,256]{1,0:T(8,128)(2,1)} %get-tuple-element.5), kind=kOutput, calls=%fused_computation.8 | convolution fusion | flops 4202496000 | bytes 14385152 | tf_op jit(solution)/shard_map/dot_general | solution.py:66
  223.5 0.2 fusion.18
  223.8 0.8 copy.49
  224.7 27.1 %all_to_all.19 = f32[1,256,2,512]{3,2,0,1:T(2,128)S(1)} all-to-all(f32[1,256,2,512]{3,2,0,1:T(2,128)S(1)} %copy.49), channel_id=1, replica_groups=mesh['op'=4,'row'=32] {'op','row'}, dimensions={1} | all-to-all | bytes 2097152 | tf_op jit(solution)/shard_map/all_to_all | solution.py:133
  251.8 0.3 copy.60
  252.1 0.9 reshape.21
  253.0 1.0 fusion.111
  254.0 0.2 fusion.51
  254.2 0.2 fusion.53
  254.4 0.2 convolution_subtract_fusion.3
  254.9 0.2 fusion.30
  255.1 0.2 fusion.57
  255.3 0.2 fusion.61
  255.5 0.2 convolution_subtract_fusion.7
  256.1 0.2 convolution_add_fusion.9
  256.3 0.2 fusion.63
  256.5 0.2 fusion.67
  256.7 0.2 convolution_add_fusion.10
  257.0 0.2 convolution_subtract_fusion.9
  257.4 0.2 convolution_subtract_fusion.6
  257.6 0.2 convolution_subtract_fusion.8
  257.8 0.2 fusion.113
  258.0 0.2 fusion.112
  258.4 0.2 fusion.69
  258.6 0.2 fusion.73
  258.8 0.2 convolution_subtract_fusion.11
  259.2 0.2 fusion.27
  259.4 0.2 convolution_add_fusion.6
  259.6 0.2 convolution_subtract_fusion.2
  259.8 0.2 fusion.119
  260.0 0.2 fusion.118
  260.2 0.2 convolution_add_fusion.7
  260.4 0.2 fusion.115
  260.6 0.2 fusion.116
  260.8 0.2 convolution_add_fusion.5
  261.0 0.2 fusion.114
  261.2 0.2 convolution_add_fusion.4
  261.4 0.2 convolution_add_fusion.8
  261.6 0.2 fusion.117
  261.8 0.2 convolution_subtract_fusion.5
  262.0 0.2 convolution_add_fusion.11
  262.2 0.2 fusion.13
  262.4 0.2 fusion.15
  262.6 0.2 fusion.14
  262.9 0.2 convolution_subtract_fusion.1
  263.1 0.2 convolution_add_fusion.1
  263.3 0.2 fusion.9
  263.5 0.2 fusion.16
  263.7 0.2 fusion.10
  264.0 0.7 pad_maximum_fusion.1
  (22 shorter events, 1.5 us)
Async XLA Ops:
  31.1 54.0 %all-to-all-start = ((bf16[32,56,2,512]{3,1,2,0:T(8,128)(2,1)}), bf16[32,56,2,512]{3,1,2,0:T(8,128)(2,1)}, u32[]{:S(2)}, u32[]{:S(2)}) async-start(bf16[32,56,2,512]{3,1,2,0:T(8,128)(2,1)} %copy.45), calls=%async_computation | async-start | bytes 7340032 | tf_op jit(solution)/shard_map/all_to_all | solution.py:50
  63.9 28.5 %copy-start.2 = (s32[125,3]{0,1:T(4,128)S(1)}, s32[125,3]{0,1:T(4,128)}, u32[]{:S(2)}) copy-start(s32[125,3]{0,1:T(4,128)} %param.6) | copy-start | bytes 4504
  63.9 28.5 %copy-start.3 = (s32[125]{0:T(128)S(1)}, s32[125]{0:T(128)}, u32[]{:S(2)}) copy-start(s32[125]{0:T(128)} %param.7) | copy-start | bytes 1504
  63.9 100.5 %copy-start.1 = (s32[256,3]{0,1:T(4,128)S(1)}, s32[256,3]{0,1:T(4,128)}, u32[]{:S(2)}) copy-start(s32[256,3]{0,1:T(4,128)} %param.8) | copy-start | bytes 9220
  85.1 112.2 %all-to-all-start.1 = ((bf16[32,69,2,512]{3,2,1,0:T(2,128)(2,1)}), bf16[32,69,2,512]{3,2,1,0:T(2,128)(2,1)}, u32[]{:S(2)}, u32[]{:S(2)}) async-start(bf16[32,69,2,512]{3,2,1,0:T(2,128)(2,1)} %copy.46), calls=%async_computation.1 | async-start | bytes 9043968 | tf_op jit(solution)/shard_map/all_to_all | solution.py:50
  224.6 29.4 %copy-start = (bf16[2,2,64,128]{3,2,1,0:T(8,128)(2,1)S(1)}, bf16[2,2,64,128]{3,2,1,0:T(8,128)(2,1)}, u32[]{:S(2)}) copy-start(bf16[2,2,64,128]{3,2,1,0:T(8,128)(2,1)} %param.9) | copy-start | bytes 196612
where the time goes:
time: 266 us; the launch traced here: 265 us
  blocking collectives  99 us (37%)
  local copies, waits for them, and re-layouts  71.9 us (27%)
  other arithmetic  38.6 us (15%)
  waiting for transfers between devices  21.3 us (8%)
  matrix products  17.5 us (7%)
  starting transfers between devices  15.9 us (6%)
    all_gather x1, blocking collectives, in_one_piece(): whole = lax.all_gather(both, axis, axis=dim, tiled=True)  71.8 us
    split x3, local copies, waits for them, and re-layouts, several_exchanges(): jnp.split(parts, piece_ends(parts.shape[widest], pieces), axis=widest)  32.6 us
    all_to_all x1, blocking collectives, on_device(): lax.all_to_all(local_sums, ('op', 'row'), split_axis=1, concat_axis=0, ti...  27.1 us
    dynamic_slice x2, local copies, waits for them, and re-layouts, on_device(): lax.dynamic_index_in_dim(wannier_ops, component // 2, 0, keepdims=False)  22.7 us
    all_to_all x2, waiting for transfers between devices, several_exchanges(): lax.all_to_all(section, axis, split_axis=0, concat_axis=0, tiled=True)  21.3 us
    convert_element_type x1, other arithmetic, make_phases(): jnp.where(derive, -along_x * sine_part, cosine).astype(jnp.bfloat16)  20.3 us
    all_to_all x2, starting transfers between devices, several_exchanges(): lax.all_to_all(section, axis, split_axis=0, concat_axis=0, tiled=True)  15.9 us
    concatenate x1, other arithmetic, several_exchanges(): return joined_along(jnp.concatenate(gathered, axis=widest), concat_dim)  12.2 us
  transfers between devices with their start and end apart: 2, of which 1 were waited for; matrix products, arithmetic and copies ran while one was open for 22% of the time, Pallas kernels for 0%

commit v1 on v0

v1 whole, which is shorter than its diff:
```python
import functools

import jax
import jax.numpy as jnp
from jax import lax
from jax.experimental import pallas as pl
from jax.experimental.pallas import tpu as pltpu
from jax.sharding import PartitionSpec as P

MESH = pl.DeviceIdType.MESH
HIGH = lax.Precision.HIGHEST
F32 = jnp.float32
BF16 = jnp.bfloat16

NR_LOC = 125
HALVES = ((0, 64), (64, 61))
BANDS = 64
FACTOR = 1.0 / 8.0
S0, S1, S2, S3 = 0.392698743691337, -0.010092707352671412, 7.766394538597307e-05, -2.6791896176843414e-07


def nt(a, b, precision=None):
    return lax.dot_general(
        a, b, (((1,), (1,)), ((), ())), preferred_element_type=F32, precision=precision
    )


def mm(a, b, precision=None):
    return jnp.dot(a, b, preferred_element_type=F32, precision=precision)


def kernel(words_ref, kp_ref, v_ref, ops_ref, out_ref, rw, rd, perm, kq, ph, tb, acc, sb, r2,
           s3, r3, fs, w_send, w_recv, d_send, d_recv, l_sem, send2, recv2, send3, recv3):
    z = lax.axis_index("op")
    row = lax.axis_index("row")
    y, x, c = row // 8, (row // 2) % 4, row % 2
    nc = 1 - c
    along = x * nc + y * c
    across = y * nc + x * c
    slot_x = x * 2 + c
    slot_y = y * 2 + c

    def dev(yy, xx, cc):
        return yy * 8 + xx * 2 + cc

    for s in range(8):
        rd[s, pl.ds(NR_LOC, 3)] = jnp.zeros((3, 2, 8, 128), BF16)

    barrier = pltpu.get_barrier_semaphore()
    me_line = z * 8 + x * 2 + c

    def greet_y(j, carry):
        o = (me_line + j) % 32
        pl.semaphore_signal(barrier, inc=1, device_id=(o // 8, y * 8 + o % 8), device_id_type=MESH)
        return carry

    def greet_x(j, carry):
        yy = (y + 1 + j // 8) % 4
        pl.semaphore_signal(
            barrier, inc=1, device_id=((j // 2) % 4, dev(yy, x, j % 2)), device_id_type=MESH
        )
        return carry

    lax.fori_loop(1, 32, greet_y, 0)
    lax.fori_loop(0, 24, greet_x, 0)
    pl.semaphore_wait(barrier, 55)

    def word_copy(k, slot, target):
        return pltpu.make_async_remote_copy(
            src_ref=words_ref, dst_ref=rw.at[slot], send_sem=w_send.at[k],
            recv_sem=w_recv.at[slot], device_id=target, device_id_type=MESH,
        )

    def data_src(tile, h):
        start, size = HALVES[h]
        return ops_ref.at[z // 2, pl.ds(start, size), :, tile]

    def data_dst(slot, h):
        start, size = HALVES[h]
        return rd.at[slot, pl.ds(start, size)]

    def data_copy(k, slot, tile, h, target):
        return pltpu.make_async_remote_copy(
            src_ref=data_src(tile, h), dst_ref=data_dst(slot, h), send_sem=d_send.at[k, h],
            recv_sem=d_recv.at[slot, h], device_id=target, device_id_type=MESH,
        )

    base = (z % 2) * 8
    peers = []
    for j in (1, 3, 2):
        xx = (x + j) % 4
        yy = (y + j) % 4
        peers.append((slot_x, base + xx, (z, dev(y, xx, 0))))
        peers.append((slot_y, base + 4 + yy, (z, dev(yy, x, 1))))
    partner_slot = slot_x * c + slot_y * nc
    partner_tile = base + nc * 4 + x * c + y * nc
    peers.append((partner_slot, partner_tile, (z, dev(y, x, nc))))
    own_slot = along * 2 + c
    own_tile = base + c * 4 + along

    for k, (slot, tile, target) in enumerate(peers):
        word_copy(k, slot, target).start()
    order = [(0, 0), (1, 0), (2, 0), (3, 0), (6, 0), (0, 1), (1, 1), (2, 1), (3, 1), (6, 1),
             (4, 0), (5, 0), (4, 1), (5, 1)]
    for k, h in order:
        slot, tile, target = peers[k]
        data_copy(k, slot, tile, h, target).start()
    for h in range(2):
        pltpu.make_async_copy(data_src(own_tile, h), data_dst(own_slot, h), l_sem.at[h]).start()
    own_words = pltpu.make_async_copy(words_ref, rw.at[own_slot], l_sem.at[2])
    own_words.start()

    o_i = lax.broadcasted_iota(jnp.int32, (256, 256), 0)
    i_i = lax.broadcasted_iota(jnp.int32, (256, 256), 1)
    perm[...] = jnp.where(i_i == (o_i % 32) * 8 + o_i // 32, 1.0, 0.0).astype(BF16)

    m_i = lax.broadcasted_iota(jnp.int32, (1024, 256), 0)
    g_i, o32 = m_i // 256, (m_i // 8) % 32
    zc = (o32 // 8) * 32 + o32 % 2
    a_i = (o32 // 2) % 4
    owner = zc + (g_i * 8 + a_i * 2) * nc + (a_i * 8 + g_i * 2) * c
    k_i = owner * 2 + (m_i // 4) % 2
    pick = jnp.where(lax.broadcasted_iota(jnp.int32, (1024, 256), 1) == k_i, 1.0, 0.0).astype(BF16)
    kxyz = mm(pick, kp_ref[...])
    m_l = lax.broadcasted_iota(jnp.int32, (1024, 128), 0)
    lane = lax.broadcasted_iota(jnp.int32, (1024, 128), 1)
    turns = (4 * (((m_l // 2) % 2 + 3 * (m_l % 2)) % 4)).astype(F32)
    kq[...] = jnp.where(lane < 3, kxyz, jnp.where(lane == 3, turns, jnp.where(lane == 4, 1.0, 0.0))).astype(BF16)

    own_words.wait()
    for slot in range(8):
        @pl.when(slot != own_slot)
        def _():
            word_copy(0, slot, (z, row)).wait_recv()

    r_row = lax.broadcasted_iota(jnp.int32, (128, 128), 0)
    r_lane = lax.broadcasted_iota(jnp.int32, (128, 128), 1)
    comp_row = (lax.broadcasted_iota(jnp.int32, (256, 128), 0) // 2) % 2 == 1
    quarter = jnp.where(r_lane >= 64, 4.0, 0.0)

    def phases(i, carry):
        slot, h = i // 2, i % 2
        word = rw[slot, pl.ds(h, 1)]
        rx = (word % 32 - 8).astype(F32)
        ry = ((word // 32) % 32 - 8).astype(F32)
        rz = ((word // 1024) % 32 - 8).astype(F32)
        deg = (word // 32768).astype(F32)
        weight = jnp.where(deg > 0.0, 1.0 / jnp.maximum(deg, 1.0), 0.0)
        along_x = rx * 0.125
        rmat = jnp.where(r_row == 0, rx, jnp.where(r_row == 1, ry, jnp.where(r_row == 2, rz, jnp.where(
            r_row == 3, 1.0, jnp.where(r_row == 4, quarter, 0.0))))).astype(BF16)
        step = (slot // 2) * 2 + h
        col = pl.multiple_of((slot % 2) * 128, 128)

        def block(b, cc):
            rows = pl.ds(pl.multiple_of(b * 256, 256), 256)
            u = mm(kq[rows, :], rmat)
            u = u - 16.0 * jnp.floor(u * 0.0625)
            t = jnp.abs(u - 8.0) - 4.0
            s = t * t
            v = t * (S0 + s * (S1 + s * (S2 + s * S3))) * weight
            v = jnp.where(comp_row, v * along_x, v)
            ph[step, rows, pl.ds(col, 128)] = v.astype(BF16)
            return cc

        lax.fori_loop(0, 4, block, 0)
        return carry

    lax.fori_loop(0, 16, phases, 0)

    def wait_data(chip, h):
        for cc in range(2):
            slot = chip * 2 + cc

            @pl.when(slot == own_slot)
            def _():
                pltpu.make_async_copy(data_src(own_tile, h), data_dst(slot, h), l_sem.at[h]).wait()

            @pl.when(slot != own_slot)
            def _():
                data_copy(0, slot, own_tile, h, (z, row)).wait_recv()

    def regroup(chip, h):
        for cc in range(2):
            for q in range(2):
                at = pl.ds(h * 64 + q * 32, 32)
                both = jnp.concatenate(
                    [rd[chip * 2 + cc, at, p].reshape(256, 128) for p in range(2)], axis=1
                )
                out = mm(perm[...], both).astype(BF16)
                for p in range(2):
                    for r in range(8):
                        tb[pl.ds(cc * 128 + p * 64 + q * 32, 32), pl.ds(r * 128, 128)] = out[
                            r * 32:(r + 1) * 32, p * 128:(p + 1) * 128
                        ]

    steps = [(0, 0), (0, 1), (1, 0), (3, 0), (1, 1), (3, 1), (2, 0), (2, 1)]
    for n, (off, h) in enumerate(steps[:-1]):
        chip = (along + off) % 4
        wait_data(chip, h)
        regroup(chip, h)

        def add(b, carry):
            rows = pl.ds(pl.multiple_of(b * 256, 256), 256)
            term = mm(ph[chip * 2 + h, rows, :], tb[...])
            if n == 0:
                acc[rows, :] = term
            else:
                acc[rows, :] = acc[rows, :] + term
            return carry

        lax.fori_loop(0, 4, add, 0)

    off, h = steps[-1]
    chip = (along + off) % 4
    wait_data(chip, h)
    regroup(chip, h)

    def partial_copy(g):
        yy, xx = g * nc + y * c, x * nc + g * c
        return pltpu.make_async_remote_copy(
            src_ref=sb.at[g], dst_ref=r2.at[across], send_sem=send2.at[g],
            recv_sem=recv2.at[across], device_id=(z, dev(yy, xx, c)), device_id_type=MESH,
        )

    def partial_from(g):
        return pltpu.make_async_remote_copy(
            src_ref=sb.at[g], dst_ref=r2.at[g], send_sem=send2.at[g],
            recv_sem=recv2.at[g], device_id=(z, row), device_id_type=MESH,
        )

    groups = [(across + j) % 4 for j in (2, 1, 3, 0)]
    for n, g in enumerate(groups):
        rows = pl.ds(pl.multiple_of(g * 256, 256), 256)
        term = acc[rows, :] + mm(ph[chip * 2 + h, rows, :], tb[...])
        if n < 3:
            sb[g] = term.astype(BF16)
        else:
            acc[rows, :] = term
        if n > 0:
            partial_copy(groups[n - 1]).start()

    for n in (1, 2, 0):
        partial_from(groups[n]).wait_recv()

    def owner_copy(o, slot):
        zz, aa, cc = o // 8, (o // 2) % 4, o % 2
        yy, xx = y * nc + aa * c, aa * nc + x * c
        return pltpu.make_async_remote_copy(
            src_ref=s3.at[o], dst_ref=r3.at[slot], send_sem=send3.at[o],
            recv_sem=recv3.at[slot], device_id=(zz, dev(yy, xx, cc)), device_id_type=MESH,
        )

    me_o = z * 8 + along * 2 + c
    my_slot = z * 8 + c * 4 + along

    def finish(b):
        rows = pl.ds(pl.multiple_of(across * 256 + b * 64, 64), 64)
        part = pl.ds(pl.multiple_of(b * 64, 64), 64)
        total = acc[rows, :]
        for n in range(3):
            total = total + r2[groups[n], part, :].astype(F32)
        s3[pl.ds(b * 8, 8)] = total.reshape(8, 8, 1024).astype(BF16)

    def send_block(b):
        def one(i, carry):
            o = b * 8 + i

            @pl.when(o != me_o)
            def _():
                owner_copy(o, my_slot).start()
            return carry

        lax.fori_loop(0, 8, one, 0)

    blocks = [(z + j) % 4 for j in (2, 1, 3, 0)]
    for n, b in enumerate(blocks):
        finish(b)
        if n > 0:
            send_block(blocks[n - 1])
    send_block(blocks[3])
    own3 = pltpu.make_async_copy(s3.at[me_o], r3.at[my_slot], l_sem.at[3])
    own3.start()
    own3.wait()

    def collect(slot, carry):
        @pl.when(slot != my_slot)
        def _():
            owner_copy(slot, slot).wait_recv()

        op, t = slot // 16, slot % 16
        for r in range(8):
            fs[pl.ds(op * 1024 + t * 8 + r, 8, stride=128), :] = r3[slot, :, r * 128:(r + 1) * 128].astype(F32)
        return carry

    lax.fori_loop(0, 32, collect, 0)

    for k2 in range(2):
        vs = v_ref[k2].reshape(128, 128)
        sums = []
        for j in range(4):
            for ri in range(2):
                at = ((j // 2) * 8 + k2 * 4 + (j % 2) * 2 + ri) * 128
                sums.append(fs[at:at + 128, :].astype(BF16))
        left = mm(vs, jnp.concatenate(sums, axis=1))
        parts = []
        for j in range(4):
            lr = left[:, (2 * j) * 128:(2 * j + 1) * 128]
            li = left[:, (2 * j + 1) * 128:(2 * j + 2) * 128]
            parts.append(lr[:64] + li[64:])
            parts.append(li[:64] - lr[64:])
        stack = jnp.concatenate(parts, axis=0)
        high = stack.astype(BF16)
        low = (stack - high.astype(F32)).astype(BF16)
        vr, vi = v_ref[k2, 0], v_ref[k2, 1]
        yr = nt(high, vr) + nt(low, vr)
        yi = nt(high, vi) + nt(low, vi)
        res = []
        for j in range(4):
            a, b = slice(128 * j, 128 * j + 64), slice(128 * j + 64, 128 * j + 128)
            res.append((yr[a] - yi[b], yi[a] + yr[b]))
        (hr, hi), (dr, di), (ar, ai), (er, ei) = res
        qr, qi = hr - di, hi + dr
        pr, pi = hr + di, hi - dr
        gr = mm(ar, qr, HIGH) - mm(ai, qi, HIGH) + mm(pr, ar, HIGH) - mm(pi, ai, HIGH)
        gi = mm(ar, qi, HIGH) + mm(ai, qr, HIGH) + mm(pr, ai, HIGH) + mm(pi, ar, HIGH)
        out_ref[k2, 0] = er + FACTOR * gr
        out_ref[k2, 1] = ei + FACTOR * gi

    for k, (slot, tile, target) in enumerate(peers):
        word_copy(k, slot, target).wait_send()
        for h in range(2):
            data_copy(k, slot, tile, h, target).wait_send()
    for g in groups[:3]:
        partial_copy(g).wait_send()

    def drain(o, carry):
        @pl.when(o != me_o)
        def _():
            owner_copy(o, my_slot).wait_send()
        return carry

    lax.fori_loop(0, 32, drain, 0)


def on_device(wannier_ops, r_coords, degeneracy, kpoints, bloch_vectors):
    ops = wannier_ops.reshape(2, NR_LOC, 2, 16, 8, 128)
    shifted = r_coords + 8
    word = shifted[:, 0] + shifted[:, 1] * 32 + shifted[:, 2] * 1024 + degeneracy * 32768
    word = jnp.pad(word, (0, 128 - NR_LOC)).reshape(2, 64)
    words = jnp.concatenate([word, word], axis=1)
    kp = jnp.pad(kpoints, ((0, 0), (0, 125))).astype(BF16)
    dma = pltpu.SemaphoreType.DMA
    res = pl.pallas_call(
        kernel,
        out_shape=jax.ShapeDtypeStruct((2, 2, BANDS, BANDS), F32),
        in_specs=[pl.BlockSpec(memory_space=pltpu.VMEM)] * 3 + [pl.BlockSpec(memory_space=pl.ANY)],
        out_specs=pl.BlockSpec(memory_space=pltpu.VMEM),
        scratch_shapes=[
            pltpu.VMEM((8, 2, 128), jnp.int32),
            pltpu.VMEM((8, 128, 2, 8, 128), BF16),
            pltpu.VMEM((256, 256), BF16),
            pltpu.VMEM((1024, 128), BF16),
            pltpu.VMEM((8, 1024, 256), BF16),
            pltpu.VMEM((256, 1024), BF16),
            pltpu.VMEM((1024, 1024), F32),
            pltpu.VMEM((4, 256, 1024), BF16),
            pltpu.VMEM((4, 256, 1024), BF16),
            pltpu.VMEM((32, 8, 1024), BF16),
            pltpu.VMEM((32, 8, 1024), BF16),
            pltpu.VMEM((2048, 128), F32),
            dma((7,)), dma((8,)), dma((7, 2)), dma((8, 2)), dma((4,)),
            dma((4,)), dma((4,)), dma((32,)), dma((32,)),
        ],
        compiler_params=pltpu.CompilerParams(
            collective_id=0, has_side_effects=True, vmem_limit_bytes=48 * 1024 * 1024
        ),
    )(words, kp, bloch_vectors, ops)
    return res.reshape(2, 2, BANDS * BANDS)


def solution(mesh):
    in_specs = (
        P(None, "row", None, None, None),
        P("row", None),
        P("row"),
        P(),
        P(("op", "row"), None, None, None),
    )
    return jax.shard_map(
        on_device, mesh=mesh, in_specs=in_specs, out_specs=P(("op", "row"), None, None), check_vma=False
    )
```

time: 266 us -> 68.5 us (0.26)
  blocking collectives: 99 us -> 0 us
  local copies, waits for them, and re-layouts: 71.9 us -> 1.83 us
  Pallas kernels: 0 us -> 64.3 us
  other arithmetic: 38.6 us -> 2.11 us
  waiting for transfers between devices: 21.3 us -> 0 us
  matrix products: 17.5 us -> 0 us
  starting transfers between devices: 15.9 us -> 0 us
    all_gather x1 -> x0, blocking collectives: 71.8 us -> none  [in_one_piece(): whole = lax.all_gather(both, axis, axis=dim, tiled=True)]
    pallas_call x0 -> x1, Pallas kernels: none -> 64.3 us  [on_device(): pl.pallas_call(kernel, out_shape=jax.ShapeDtypeStruct((2, 2, BANDS, BANDS...]
    split x3 -> x0, local copies, waits for them, and re-layouts: 32.6 us -> none  [several_exchanges(): jnp.split(parts, piece_ends(parts.shape[widest], pieces), axis=widest)]
    all_to_all x1 -> x0, blocking collectives: 27.1 us -> none  [on_device(): lax.all_to_all(local_sums, ('op', 'row'), split_axis=1, concat_axis=0, ti...]
    dynamic_slice x2 -> x0, local copies, waits for them, and re-layouts: 22.7 us -> none  [on_device(): lax.dynamic_index_in_dim(wannier_ops, component // 2, 0, keepdims=False)]
    all_to_all x2 -> x0, waiting for transfers between devices: 21.3 us -> none  [several_exchanges(): lax.all_to_all(section, axis, split_axis=0, concat_axis=0, tiled=True)]
    convert_element_type x1 -> x0, other arithmetic: 20.3 us -> none  [make_phases(): jnp.where(derive, -along_x * sine_part, cosine).astype(jnp.bfloat16)]
    dot_general x49 -> x0, matrix products: 17.5 us -> none  [the longest x48 9.37 us: single(): return jnp.einsum(form, first, second, precision=HIGH)]
  transfers between devices with their start and end apart: 2 -> 0, of which waited for: 1 -> 0; matrix products, arithmetic and copies ran while one was open for 22% -> 0% of each run, Pallas kernels for 0% -> 0%
where the time goes in v1:
time: 68.5 us; the launch traced here: 68.3 us
  Pallas kernels  64.3 us (94%)
  other arithmetic  2.11 us (3%)
  local copies, waits for them, and re-layouts  1.83 us (3%)
    pallas_call x1, Pallas kernels, on_device(): pl.pallas_call(kernel, out_shape=jax.ShapeDtypeStruct((2, 2, BANDS, BANDS...  64.3 us

profile of v1, /device:TPU:1, one launch (start us, length us, event | category | flops | bytes accessed | tf_op | source)
XLA Modules:
  0.0 68.3 jit_solution(13505007777287960517)
XLA Ops:
  0.0 0.7 %broadcast_add_fusion = s32[125,3]{0,1:T(4,128)S(1)} fusion(s32[125,3]{0,1:T(4,128)} %param.6), kind=kLoop, calls=%fused_computation.1 | loop fusion | flops 375 | bytes 3000 | tf_op jit(solution)/shard_map/add | solution.py:348
  0.7 0.7 bitcast_add_fusion
  1.4 0.1 reshape.15
  1.4 0.1 pad_add_fusion.words_ref
  1.5 0.7 %convert.4 = bf16[256,3]{0,1:T(4,128)(2,1)S(1)} convert(s32[256,3]{0,1:T(4,128)} %param.8) | non-fusion elementwise | flops 768 | bytes 4608 | tf_op jit(solution)/shard_map/convert
  2.2 0.1 copy.7
  2.4 0.0 copy-start
  2.4 0.8 %copy-done = bf16[2,2,64,128]{3,2,1,0:T(8,128)(2,1)S(1)} copy-done((bf16[2,2,64,128]{3,2,1,0:T(8,128)(2,1)S(1)}, bf16[2,2,64,128]{3,2,1,0:T(8,128)(2,1)}, u32[]{:S(2)}) %copy-start) | copy-done | bytes 65560
  3.2 64.3 %shard_map.55 = f32[2,2,64,64]{3,2,1,0:T(8,128)S(1)} custom-call(s32[2,128]{1,0:T(2,128)S(1)} %pad_add_fusion.words_ref, bf16[256,128]{1,0:T(8,128)(2,1)S(1)} %pad.10.kp_ref, bf16[2,2,64,128]{3,2,1,0:T(8,128)(2,1)S(1)} %copy-done, bf16[2,125,2,16,8,128]{5,4,3,2,1,0:T(8,128)(2,1)} %bitcast.5), custom_call_target="tpu_custom_call" | custom-call | tf_op jit(solution)/shard_map/pallas_call | solution.py:354
  67.5 0.7 %reshape.17 = f32[2,2,4096]{2,1,0:T(2,128)} reshape(f32[2,2,64,64]{3,2,1,0:T(8,128)S(1)} %shard_map.55) | data formatting | bytes 131072 | tf_op jit(solution)/shard_map/reshape | solution.py:379
  (2 shorter events, 0.0 us)
Async XLA Ops:
  2.4 0.8 %copy-start = (bf16[2,2,64,128]{3,2,1,0:T(8,128)(2,1)S(1)}, bf16[2,2,64,128]{3,2,1,0:T(8,128)(2,1)}, u32[]{:S(2)}) copy-start(bf16[2,2,64,128]{3,2,1,0:T(8,128)(2,1)} %v_ref.1) | copy-start | bytes 196612

commit v2 on v1

v2 whole, which is shorter than its diff:
```python
import jax
import jax.numpy as jnp
from jax import lax
from jax.experimental import pallas as pl
from jax.experimental.pallas import tpu as pltpu
from jax.sharding import PartitionSpec as P

MESH = pl.DeviceIdType.MESH
HIGH = lax.Precision.HIGHEST
F32 = jnp.float32
BF16 = jnp.bfloat16
I32 = jnp.int32

NR_LOC = 125
SIZES = (64, 61)
PASSES = 2
ROWS = 8 // PASSES
WIDE = ROWS * 128
GROUP = 256 // ROWS
BANDS = 64
FACTOR = 1.0 / 8.0
S0 = 0.392698743691337 * 16.0
S1 = -0.010092707352671412 * 16.0 ** 3
S2 = 7.766394538597307e-05 * 16.0 ** 5
S3 = -2.6791896176843414e-07 * 16.0 ** 7
MAGIC = 12582912.0


def nt(a, b, precision=None):
    return lax.dot_general(
        a, b, (((1,), (1,)), ((), ())), preferred_element_type=F32, precision=precision
    )


def mm(a, b, precision=None):
    return jnp.dot(a, b, preferred_element_type=F32, precision=precision)


def iota(shape, dim):
    return lax.broadcasted_iota(I32, shape, dim)


def kernel(coord_ref, deg_ref, kp_ref, v_ref, ops_ref, out_ref, rc, rg, rd, kps, vs_ref, perm, pick,
           kpp, kq, cm, wx, rmat, ph, tb, acc, sb, r2, s3, r3, fs, c_send, c_recv, g_send, g_recv,
           d_send, d_recv, l_sem, send2, recv2, send3, recv3):
    z = lax.axis_index("op")
    row = lax.axis_index("row")
    y, x, c = row // 8, (row // 2) % 4, row % 2
    nc = 1 - c
    along = x * nc + y * c
    across = y * nc + x * c
    slot_x = x * 2 + c
    slot_y = y * 2 + c

    def dev(yy, xx, cc):
        return yy * 8 + xx * 2 + cc

    for p in range(PASSES):
        for s in range(8):
            rd[p, s, pl.ds(NR_LOC, 3)] = jnp.zeros((3, 2, ROWS, 128), BF16)

    barrier = pltpu.get_barrier_semaphore()

    def greet(zz, rr):
        pl.semaphore_signal(barrier, inc=1, device_id=(zz, rr), device_id_type=MESH)

    for j in (2, 1, 3):
        yy, xx, zz = (y + j) % 4, (x + j) % 4, (z + j) % 4
        near = dev(y * nc + yy * c, xx * nc + x * c, 0)
        greet(z, near)
        greet(z, near + 1)
        greet(z, dev(yy * nc + y * c, x * nc + xx * c, c))
        greet(zz, row)
    greet(z, dev(y, x, nc))

    base = (z % 2) * 8

    def data_src(tile, p, h):
        return ops_ref.at[z // 2, pl.ds(64 * h, SIZES[h]), :, tile, p]

    def data_dst(slot, p, h):
        return rd.at[p, slot, pl.ds(64 * h, SIZES[h])]

    def data_copy(k, slot, tile, p, h, target):
        return pltpu.make_async_remote_copy(
            src_ref=data_src(tile, p, h), dst_ref=data_dst(slot, p, h), send_sem=d_send.at[k, p, h],
            recv_sem=d_recv.at[slot, p, h], device_id=target, device_id_type=MESH,
        )

    own_slot = along * 2 + c
    own_tile = base + c * 4 + along

    def own_data(p, h):
        return pltpu.make_async_copy(
            data_src(own_tile, p, h), data_dst(own_slot, p, h), d_recv.at[own_slot, p, h]
        )

    kp_copy = pltpu.make_async_copy(kp_ref, kps, l_sem.at[0])
    v_copy = pltpu.make_async_copy(v_ref, vs_ref, l_sem.at[1])
    own_coord = pltpu.make_async_copy(coord_ref, rc.at[own_slot], c_recv.at[own_slot])
    own_deg = pltpu.make_async_copy(deg_ref, rg.at[own_slot], g_recv.at[own_slot])
    for copy in (kp_copy, own_coord, own_deg, v_copy):
        copy.start()
    for p in range(PASSES):
        for h in range(2):
            own_data(p, h).start()

    m_i = iota((1024, 128), 0)
    lane = iota((1024, 128), 1)
    g_i, o32 = m_i // 256, (m_i // 8) % 32
    a_i = (o32 // 2) % 4
    owner = (o32 // 8) * 32 + o32 % 2 + (g_i * 8 + a_i * 2) * nc + (a_i * 8 + g_i * 2) * c
    k_i = owner * 2 + (m_i // 4) % 2
    for half in range(2):
        pick[:, half * 128:(half + 1) * 128] = jnp.where(lane + 128 * half == k_i, 1.0, 0.0).astype(BF16)

    peers = []
    for j in (1, 3, 2):
        xx = (x + j) % 4
        yy = (y + j) % 4
        peers.append((slot_x, base + xx, (z, dev(y, xx, 0))))
        peers.append((slot_y, base + 4 + yy, (z, dev(yy, x, 1))))
    peers.append((slot_x * c + slot_y * nc, base + nc * 4 + x * c + y * nc, (z, dev(y, x, nc))))

    def coord_copy(k, slot, target):
        return pltpu.make_async_remote_copy(
            src_ref=coord_ref, dst_ref=rc.at[slot], send_sem=c_send.at[k],
            recv_sem=c_recv.at[slot], device_id=target, device_id_type=MESH,
        )

    def deg_copy(k, slot, target):
        return pltpu.make_async_remote_copy(
            src_ref=deg_ref, dst_ref=rg.at[slot], send_sem=g_send.at[k],
            recv_sem=g_recv.at[slot], device_id=target, device_id_type=MESH,
        )

    pl.semaphore_wait(barrier, 13)
    for k, (slot, tile, target) in enumerate(peers):
        coord_copy(k, slot, target).start()
        deg_copy(k, slot, target).start()
    order = [(0, 0), (1, 0), (2, 0), (3, 0), (6, 0), (0, 1), (1, 1), (2, 1), (3, 1), (6, 1),
             (4, 0), (5, 0), (4, 1), (5, 1)]
    for p in range(PASSES):
        for k, h in order:
            slot, tile, target = peers[k]
            data_copy(k, slot, tile, p, h, target).start()

    o_i, i_i = iota((256, 256), 0), iota((256, 256), 1)
    perm[...] = jnp.where(i_i == (o_i % GROUP) * ROWS + o_i // GROUP, 1.0, 0.0).astype(BF16)

    kpp[...] = jnp.zeros(kpp.shape, F32)
    kp_copy.wait()
    kpp[0:3, :] = kps[...].astype(F32)
    kxyz = nt(pick[...], kpp[...].astype(BF16))
    turns = (((m_i // 2) % 2 + 3 * (m_i % 2)) % 4).astype(F32) * 0.25
    kq[...] = jnp.where(lane < 3, kxyz, jnp.where(lane == 3, turns, jnp.where(lane == 4, 1.0, 0.0))).astype(BF16)

    cm[...] = jnp.zeros(cm.shape, F32)
    rmat[...] = jnp.zeros(rmat.shape, BF16)
    own_coord.wait()
    own_deg.wait()
    for slot in range(8):
        @pl.when(slot != own_slot)
        def _():
            coord_copy(0, slot, (z, row)).wait_recv()
            deg_copy(0, slot, (z, row)).wait_recv()

        cm[slot * 8:slot * 8 + 3, 0:NR_LOC] = rc[slot].astype(F32)
        cm[slot * 8 + 3:slot * 8 + 4, 0:NR_LOC] = rg[slot].astype(F32)
    s_r, s_l = iota((128, 256), 0), iota((128, 256), 1)
    spread = jnp.where(s_r == (s_l // 128) * 64 + s_l % 64, 1.0, 0.0).astype(BF16)
    wx[...] = mm(cm[...].astype(BF16), spread)

    row8, lane8 = iota((8, 128), 0), iota((8, 128), 1)
    quarter = jnp.where(lane8 >= 64, 0.25, 0.0)

    def phases(i, carry):
        chip, h = i // 2, i % 2
        amps = []
        for cc in range(2):
            blk = wx[pl.ds(pl.multiple_of((chip * 2 + cc) * 8, 8), 8), pl.ds(pl.multiple_of(h * 128, 128), 128)]
            deg = blk[3:4]
            weight = jnp.where(deg > 0.0, 1.0 / jnp.maximum(deg, 1.0), 0.0)
            moment = weight * (blk[0:1] * 0.125)
            amps.append(jnp.where((row8 // 2) % 2 == 1, moment, weight))
            top = jnp.where(row8 < 3, blk * 0.0625, jnp.where(row8 == 3, 1.0, jnp.where(row8 == 4, quarter, 0.0)))
            rmat[0:16, cc * 128:(cc + 1) * 128] = jnp.concatenate([top, jnp.zeros((8, 128), F32)], axis=0).astype(BF16)
        amp = jnp.concatenate(amps, axis=1)

        def block(b, cc):
            rows = pl.ds(pl.multiple_of(b * 256, 256), 256)
            u = mm(kq[rows, :], rmat[...])
            u = u - ((u + MAGIC) - MAGIC)
            t = 0.25 - jnp.abs(u)
            s = t * t
            v = t * (S0 + s * (S1 + s * (S2 + s * S3)))
            v = (v.reshape(32, 8, 256) * amp[None]).reshape(256, 256)
            ph[i, rows, :] = v.astype(BF16)
            return cc

        lax.fori_loop(0, 4, block, 0)
        return carry

    lax.fori_loop(0, 8, phases, 0)

    def gather(p, i):
        off = jnp.where(i < 2, 0, jnp.where(i >= 6, 2, 1 + 2 * (i % 2)))
        h = jnp.where(i < 2, i, jnp.where(i < 4, 0, jnp.where(i < 6, 1, i - 6)))
        chip = (along + off) % 4
        for cc in range(2):
            slot = chip * 2 + cc
            for hh in range(2):
                @pl.when(h == hh)
                def _():
                    @pl.when(slot == own_slot)
                    def _():
                        own_data(p, hh).wait()

                    @pl.when(slot != own_slot)
                    def _():
                        data_copy(0, slot, own_tile, p, hh, (z, row)).wait_recv()

            for q in range(64 // GROUP):
                at = pl.ds(h * 64 + q * GROUP, GROUP)
                both = jnp.concatenate(
                    [rd[p, slot, at, part].reshape(256, 128) for part in range(2)], axis=1
                )
                out = mm(perm[...], both).astype(BF16)
                for part in range(2):
                    for r in range(ROWS):
                        tb[pl.ds(cc * 128 + part * 64 + q * GROUP, GROUP), pl.ds(r * 128, 128)] = out[
                            r * GROUP:(r + 1) * GROUP, part * 128:(part + 1) * 128
                        ]
        return chip * 2 + h

    def partial_copy(p, g):
        yy, xx = g * nc + y * c, x * nc + g * c
        return pltpu.make_async_remote_copy(
            src_ref=sb.at[p, g], dst_ref=r2.at[p, across], send_sem=send2.at[p, g],
            recv_sem=recv2.at[p, across], device_id=(z, dev(yy, xx, c)), device_id_type=MESH,
        )

    def partial_from(p, g):
        return pltpu.make_async_remote_copy(
            src_ref=sb.at[p, g], dst_ref=r2.at[p, g], send_sem=send2.at[p, g],
            recv_sem=recv2.at[p, g], device_id=(z, row), device_id_type=MESH,
        )

    groups = [(across + j) % 4 for j in (2, 1, 3)]

    for p in range(PASSES):
        acc[p] = jnp.zeros(acc.shape[1:], F32)

        def step(i, carry):
            at = gather(p, i)
            for n in range(WIDE // 256):
                cols = slice(n * 256, (n + 1) * 256)
                acc[p, :, cols] = acc[p, :, cols] + mm(ph[at], tb[:, cols])
            return carry

        lax.fori_loop(0, 7, step, 0)
        at = gather(p, 7)
        for n in range(WIDE // 256):
            cols = slice(n * 256, (n + 1) * 256)
            full = acc[p, :, cols] + mm(ph[at], tb[:, cols])
            acc[p, :, cols] = full
            sb[p, :, :, cols] = full.reshape(4, 256, 256).astype(BF16)
        for g in groups:
            partial_copy(p, g).start()

    def owner_copy(p, o, slot):
        zz, aa, cc = o // 8, (o // 2) % 4, o % 2
        yy, xx = y * nc + aa * c, aa * nc + x * c
        return pltpu.make_async_remote_copy(
            src_ref=s3.at[p, o], dst_ref=r3.at[p, slot], send_sem=send3.at[p, o],
            recv_sem=recv3.at[p, slot], device_id=(zz, dev(yy, xx, cc)), device_id_type=MESH,
        )

    me_o = z * 8 + along * 2 + c
    my_slot = z * 8 + c * 4 + along

    def own_sum(p):
        return pltpu.make_async_copy(s3.at[p, me_o], r3.at[p, my_slot], recv3.at[p, my_slot])

    def finish(p, b):
        rows = pl.ds(pl.multiple_of(across * 256 + b * 64, 64), 64)
        part = pl.ds(pl.multiple_of(b * 64, 64), 64)
        total = acc[p, rows, :]
        for g in groups:
            total = total + r2[p, g, part, :].astype(F32)
        s3[p, pl.ds(b * 8, 8)] = total.reshape(8, 8, WIDE).astype(BF16)

    def send_block(p, b):
        def one(i, carry):
            o = b * 8 + i

            @pl.when(o != me_o)
            def _():
                owner_copy(p, o, my_slot).start()
            return carry

        lax.fori_loop(0, 8, one, 0)

    blocks = [(z + j) % 4 for j in (2, 1, 3, 0)]
    for p in range(PASSES):
        for g in (groups[1], groups[2], groups[0]):
            partial_from(p, g).wait_recv()
        for n, b in enumerate(blocks):
            finish(p, b)
            if n > 0:
                send_block(p, blocks[n - 1])
        send_block(p, blocks[3])
        own_sum(p).start()

    for p in range(PASSES):
        own_sum(p).wait()

        def collect(slot, carry):
            @pl.when(slot != my_slot)
            def _():
                owner_copy(p, slot, slot).wait_recv()

            op, t = slot // 16, slot % 16
            for r in range(ROWS):
                fs[pl.ds(op * 1024 + t * 8 + p * ROWS + r, 8, stride=128), :] = r3[
                    p, slot, :, r * 128:(r + 1) * 128
                ].astype(F32)
            return carry

        lax.fori_loop(0, 32, collect, 0)

    v_copy.wait()
    for k2 in range(2):
        vs = vs_ref[k2].reshape(128, 128)
        sums = []
        for j in range(4):
            for ri in range(2):
                at = ((j // 2) * 8 + k2 * 4 + (j % 2) * 2 + ri) * 128
                sums.append(fs[at:at + 128, :].astype(BF16))
        left = mm(vs, jnp.concatenate(sums, axis=1))
        parts = []
        for j in range(4):
            lr = left[:, (2 * j) * 128:(2 * j + 1) * 128]
            li = left[:, (2 * j + 1) * 128:(2 * j + 2) * 128]
            parts.append(lr[:64] + li[64:])
            parts.append(li[:64] - lr[64:])
        stack = jnp.concatenate(parts, axis=0)
        high = stack.astype(BF16)
        low = (stack - high.astype(F32)).astype(BF16)
        vr, vi = vs_ref[k2, 0], vs_ref[k2, 1]
        yr = nt(high, vr) + nt(low, vr)
        yi = nt(high, vi) + nt(low, vi)
        res = []
        for j in range(4):
            a, b = slice(128 * j, 128 * j + 64), slice(128 * j + 64, 128 * j + 128)
            res.append((yr[a] - yi[b], yi[a] + yr[b]))
        (hr, hi), (dr, di), (ar, ai), (er, ei) = res
        qr, qi = hr - di, hi + dr
        pr, pi = hr + di, hi - dr
        gr = mm(ar, qr, HIGH) - mm(ai, qi, HIGH) + mm(pr, ar, HIGH) - mm(pi, ai, HIGH)
        gi = mm(ar, qi, HIGH) + mm(ai, qr, HIGH) + mm(pr, ai, HIGH) + mm(pi, ar, HIGH)
        out_ref[k2, 0] = er + FACTOR * gr
        out_ref[k2, 1] = ei + FACTOR * gi

    for k, (slot, tile, target) in enumerate(peers):
        coord_copy(k, slot, target).wait_send()
        deg_copy(k, slot, target).wait_send()
        for p in range(PASSES):
            for h in range(2):
                data_copy(k, slot, tile, p, h, target).wait_send()
    for p in range(PASSES):
        for g in groups:
            partial_copy(p, g).wait_send()

        def drain(o, carry):
            @pl.when(o != me_o)
            def _():
                owner_copy(p, o, my_slot).wait_send()
            return carry

        lax.fori_loop(0, 32, drain, 0)


def on_device(wannier_ops, r_coords, degeneracy, kpoints, bloch_vectors):
    ops = wannier_ops.reshape(2, NR_LOC, 2, 16, PASSES, ROWS, 128)
    dma = pltpu.SemaphoreType.DMA
    vmem = pltpu.VMEM
    res = pl.pallas_call(
        kernel,
        out_shape=jax.ShapeDtypeStruct((2, 2, BANDS, BANDS), F32),
        in_specs=[pl.BlockSpec(memory_space=pl.ANY)] * 5,
        out_specs=pl.BlockSpec(memory_space=vmem),
        scratch_shapes=[
            vmem((8, 3, NR_LOC), I32),
            vmem((8, 1, NR_LOC), I32),
            vmem((PASSES, 8, 128, 2, ROWS, 128), BF16),
            vmem((3, 256), I32),
            vmem((2, 2, 64, 128), BF16),
            vmem((256, 256), BF16),
            vmem((1024, 256), BF16),
            vmem((128, 256), F32),
            vmem((1024, 128), BF16),
            vmem((64, 128), F32),
            vmem((64, 256), F32),
            vmem((128, 256), BF16),
            vmem((8, 1024, 256), BF16),
            vmem((256, WIDE), BF16),
            vmem((PASSES, 1024, WIDE), F32),
            vmem((PASSES, 4, 256, WIDE), BF16),
            vmem((PASSES, 4, 256, WIDE), BF16),
            vmem((PASSES, 32, 8, WIDE), BF16),
            vmem((PASSES, 32, 8, WIDE), BF16),
            vmem((2048, 128), F32),
            dma((7,)), dma((8,)), dma((7,)), dma((8,)), dma((7, PASSES, 2)), dma((8, PASSES, 2)), dma((2,)),
            dma((PASSES, 4)), dma((PASSES, 4)), dma((PASSES, 32)), dma((PASSES, 32)),
        ],
        compiler_params=pltpu.CompilerParams(
            collective_id=0, has_side_effects=True, vmem_limit_bytes=56 * 1024 * 1024
        ),
    )(r_coords.T, degeneracy.reshape(1, NR_LOC), kpoints.T, bloch_vectors, ops)
    return res.reshape(2, 2, BANDS * BANDS)


def solution(mesh):
    in_specs = (
        P(None, "row", None, None, None),
        P("row", None),
        P("row"),
        P(),
        P(("op", "row"), None, None, None),
    )
    return jax.shard_map(
        on_device, mesh=mesh, in_specs=in_specs, out_specs=P(("op", "row"), None, None), check_vma=False
    )
```

time: 68.5 us -> 57.5 us (0.84)
  Pallas kernels: 64.3 us -> 55.7 us
  other arithmetic: 2.11 us -> 0 us
    pallas_call x1, Pallas kernels: 64.3 us -> 55.7 us  [on_device(): pl.pallas_call(kernel, out_shape=jax.ShapeDtypeStruct((2, 2, BANDS, BANDS...]
    add x2 -> x0, other arithmetic: 1.34 us -> none  [the longest x1 0.68 us: on_device(): shifted = r_coords + 8]
    reshape x1, local copies, waits for them, and re-layouts: 0.74 us -> 1.64 us  [on_device(): return res.reshape(2, 2, BANDS * BANDS)]
    unnamed x2 -> x0, local copies, waits for them, and re-layouts: 0.83 us -> none
    another operation x1 -> x0, other arithmetic: 0.69 us -> none
where the time goes in v2:
time: 57.5 us; the launch traced here: 57.4 us
  Pallas kernels  55.7 us (97%)
  local copies, waits for them, and re-layouts  1.64 us (3%)
    pallas_call x1, Pallas kernels, on_device(): pl.pallas_call(kernel, out_shape=jax.ShapeDtypeStruct((2, 2, BANDS, BANDS...  55.7 us
    reshape x1, local copies, waits for them, and re-layouts, on_device(): return res.reshape(2, 2, BANDS * BANDS)  1.64 us

profile of v2, /device:TPU:1, one launch (start us, length us, event | category | flops | bytes accessed | tf_op | source)
XLA Modules:
  0.0 57.4 jit_solution(13006974441304397673)
XLA Ops:
  0.0 55.7 %shard_map.55 = f32[2,2,64,64]{3,2,1,0:T(8,128)} custom-call(s32[3,125]{1,0:T(4,128)} %bitcast.8, s32[1,125]{1,0:T(1,128)} %bitcast.9, s32[3,256]{1,0:T(4,128)} %bitcast.7, bf16[2,2,64,128]{3,2,1,0:T(8,128)(2,1)} %v_ref.1, bf16[2,125,2,16,2,4,128]{6,5,4,3,2,1,0:T(4,128)(2,1)} %bitcast.6), custom_call_target="tpu_custom_call" | custom-call | tf_op jit(solution)/shard_map/pallas_call | solution.py:388
  55.7 1.6 %reshape.11 = f32[2,2,4096]{2,1,0:T(2,128)} reshape(f32[2,2,64,64]{3,2,1,0:T(8,128)} %shard_map.55) | data formatting | bytes 131072 | tf_op jit(solution)/shard_map/reshape | solution.py:421

commit v3 on v2

v3 whole, which is shorter than its diff:
```python
import jax
import jax.numpy as jnp
from jax import lax
from jax.experimental import pallas as pl
from jax.experimental.pallas import tpu as pltpu
from jax.sharding import PartitionSpec as P

MESH = pl.DeviceIdType.MESH
HIGH = lax.Precision.HIGHEST
F32 = jnp.float32
BF16 = jnp.bfloat16
I32 = jnp.int32

NR_LOC = 125
SIZES = (64, 61)
PASSES = 4
ROWS = 8 // PASSES
WIDE = ROWS * 128
TILES = WIDE // 256
SUB = 256
PER = WIDE // SUB
SUBS = PASSES * PER
LAG = 2 if SUBS > 2 else 1
TALL = 64 * ROWS
FACTOR = 1.0 / 8.0
S0 = 0.392698743691337 * 16.0
S1 = -0.010092707352671412 * 16.0 ** 3
S2 = 7.766394538597307e-05 * 16.0 ** 5
S3 = -2.6791896176843414e-07 * 16.0 ** 7
MAGIC = 12582912.0


def nt(a, b, precision=None):
    return lax.dot_general(
        a, b, (((1,), (1,)), ((), ())), preferred_element_type=F32, precision=precision
    )


def mm(a, b, precision=None):
    return jnp.dot(a, b, preferred_element_type=F32, precision=precision)


def iota(shape, dim):
    return lax.broadcasted_iota(I32, shape, dim)


def kernel(coord_ref, deg_ref, kp_ref, v_ref, ops_ref, out_ref, rc, rg, rd, kps, vs_ref, perm, pick,
           kpp, kq, cm, wx, rmat, tw, ph, tb, acc, sb, r2, s3, r3, fs, g, og, c_send, c_recv, g_send, g_recv,
           d_send, d_recv, l_sem, send2, recv2, send3, recv3):
    z = lax.axis_index("op")
    row = lax.axis_index("row")
    y, x, c = row // 8, (row // 2) % 4, row % 2
    nc = 1 - c
    along = x * nc + y * c
    across = y * nc + x * c
    slot_x = x * 2 + c
    slot_y = y * 2 + c

    def dev(yy, xx, cc):
        return yy * 8 + xx * 2 + cc

    def bytes_of(ref, sem):
        pltpu.make_async_copy(ref, ref, sem).wait()

    for p in range(PASSES):
        for s in range(8):
            rd[p, s, pl.ds(NR_LOC, 3)] = jnp.zeros((3, 2, ROWS, 128), BF16)

    barrier = pltpu.get_barrier_semaphore()

    def greet(zz, rr):
        pl.semaphore_signal(barrier, inc=1, device_id=(zz, rr), device_id_type=MESH)

    for j in (2, 1, 3):
        yy, xx, zz = (y + j) % 4, (x + j) % 4, (z + j) % 4
        near = dev(y * nc + yy * c, xx * nc + x * c, 0)
        greet(z, near)
        greet(z, near + 1)
        greet(z, dev(yy * nc + y * c, x * nc + xx * c, c))
        greet(zz, row)
    greet(z, dev(y, x, nc))

    base = (z % 2) * 8

    def data_src(tile, p, h):
        return ops_ref.at[z // 2, pl.ds(64 * h, SIZES[h]), :, tile, p]

    def data_dst(slot, p, h):
        return rd.at[p, slot, pl.ds(64 * h, SIZES[h])]

    def data_copy(slot, tile, p, h, target):
        return pltpu.make_async_remote_copy(
            src_ref=data_src(tile, p, h), dst_ref=data_dst(slot, p, h), send_sem=d_send,
            recv_sem=d_recv.at[slot // 2, p, h], device_id=target, device_id_type=MESH,
        )

    own_slot = along * 2 + c
    own_tile = base + c * 4 + along

    def own_data(p, h):
        return pltpu.make_async_copy(
            data_src(own_tile, p, h), data_dst(own_slot, p, h), d_recv.at[along, p, h]
        )

    kp_copy = pltpu.make_async_copy(kp_ref, kps, l_sem.at[0])
    v_copy = pltpu.make_async_copy(v_ref, vs_ref, l_sem.at[1])
    own_coord = pltpu.make_async_copy(coord_ref, rc.at[own_slot], c_recv)
    own_deg = pltpu.make_async_copy(deg_ref, rg.at[own_slot], g_recv)
    for copy in (kp_copy, own_coord, own_deg, v_copy):
        copy.start()
    for p in range(PASSES):
        for h in range(2):
            own_data(p, h).start()

    k_r, k_l = iota((256, 256), 0), iota((256, 256), 1)
    g_i, o32 = k_r // 64, (k_r // 2) % 32
    a_i = (o32 // 2) % 4
    owner = (o32 // 8) * 32 + o32 % 2 + (g_i * 8 + a_i * 2) * nc + (a_i * 8 + g_i * 2) * c
    pick[...] = jnp.where(k_l == owner * 2 + k_r % 2, 1.0, 0.0).astype(BF16)

    peers = []
    for j in (1, 3, 2):
        xx = (x + j) % 4
        yy = (y + j) % 4
        peers.append((slot_x, base + xx, (z, dev(y, xx, 0))))
        peers.append((slot_y, base + 4 + yy, (z, dev(yy, x, 1))))
    peers.append((slot_x * c + slot_y * nc, base + nc * 4 + x * c + y * nc, (z, dev(y, x, nc))))

    def coord_copy(slot, target):
        return pltpu.make_async_remote_copy(
            src_ref=coord_ref, dst_ref=rc.at[slot], send_sem=c_send,
            recv_sem=c_recv, device_id=target, device_id_type=MESH,
        )

    def deg_copy(slot, target):
        return pltpu.make_async_remote_copy(
            src_ref=deg_ref, dst_ref=rg.at[slot], send_sem=g_send,
            recv_sem=g_recv, device_id=target, device_id_type=MESH,
        )

    pl.semaphore_wait(barrier, 13)
    for slot, tile, target in peers:
        coord_copy(slot, target).start()
        deg_copy(slot, target).start()
    order = [(0, 0), (1, 0), (2, 0), (3, 0), (6, 0), (0, 1), (1, 1), (2, 1), (3, 1), (6, 1),
             (4, 0), (5, 0), (4, 1), (5, 1)]
    for p in range(PASSES):
        for k, h in order:
            slot, tile, target = peers[k]
            data_copy(slot, tile, p, h, target).start()

    o_i, i_i = iota((256, 256), 0), iota((256, 256), 1)
    p_o, p_i = iota((TALL, TALL), 0), iota((TALL, TALL), 1)
    perm[...] = jnp.where(p_i == (p_o % 64) * ROWS + p_o // 64, 1.0, 0.0).astype(BF16)

    kpp[...] = jnp.zeros(kpp.shape, F32)
    kp_copy.wait()
    kpp[0:3, :] = kps[...].astype(F32)
    kq[...] = nt(pick[...], kpp[...].astype(BF16)).astype(BF16)

    cm[...] = jnp.zeros(cm.shape, F32)
    rmat[...] = jnp.zeros(rmat.shape, BF16)
    bytes_of(rc, c_recv)
    bytes_of(rg, g_recv)
    for slot in range(8):
        at, lanes = (slot // 2) * 8, slice((slot % 2) * 128, (slot % 2) * 128 + NR_LOC)
        cm[at:at + 3, lanes] = rc[slot].astype(F32)
        cm[at + 3:at + 4, lanes] = rg[slot].astype(F32)
    s_c, s_h, s_r = (i_i % 128) // 64, i_i // 128, i_i % 64
    spread = jnp.where(o_i == s_c * 128 + s_h * 64 + s_r, 1.0, 0.0).astype(BF16)
    wx[...] = mm(cm[...].astype(BF16), spread)

    def turn_cos(u):
        u = u - ((u + MAGIC) - MAGIC)
        t = 0.25 - jnp.abs(u)
        q = t * t
        return t * (S0 + q * (S1 + q * (S2 + q * S3)))

    def phases(i, carry):
        chip, h = i // 2, i % 2
        blk = wx[pl.ds(pl.multiple_of(chip * 8, 8), 8), pl.ds(pl.multiple_of(h * 128, 128), 128)]
        deg = blk[3:4]
        weight = jnp.where(deg > 0.0, 1.0 / jnp.maximum(deg, 1.0), 0.0)
        place = blk[0:1] * 0.125
        rmat[0:16, :] = jnp.concatenate([blk * 0.0625, jnp.zeros((8, 128), F32)], axis=0).astype(BF16)

        for b in range(4):
            u = mm(kq[b * 64:(b + 1) * 64, :], rmat[...])
            cos = turn_cos(u) * weight
            sin = turn_cos(u - 0.25) * weight
            x_cos, x_sin = cos * place, sin * place
            for q, (first, second) in enumerate(((cos, -sin), (sin, cos), (-x_sin, -x_cos), (x_cos, -x_sin))):
                at = pl.ds(b * 256 + q, 64, stride=4)
                tw[0, at, :] = first
                tw[1, at, :] = second
        for b in range(4):
            rows = slice(b * 256, (b + 1) * 256)
            for part in range(2):
                ph[i, rows, part * 128:(part + 1) * 128] = tw[part, rows, :].astype(BF16)
        return carry

    lax.fori_loop(0, 8, phases, 0)

    def gather(p, i):
        off = jnp.where(i < 2, 0, jnp.where(i >= 6, 2, 1 + 2 * (i % 2)))
        h = jnp.where(i < 2, i, jnp.where(i < 4, 0, jnp.where(i < 6, 1, i - 6)))
        chip = (along + off) % 4
        for hh in range(2):
            @pl.when(h == hh)
            def _():
                bytes_of(rd.at[p, pl.ds(0, 2), pl.ds(0, SIZES[hh])], d_recv.at[chip, p, hh])

        at = pl.ds(h * 64, 64)
        blocks = [rd[p, chip * 2 + cc, at, part].reshape(TALL, 128) for part in range(2) for cc in range(2)]
        out = mm(perm[...], jnp.concatenate(blocks, axis=1)).astype(BF16)
        for n in range(4):
            for r in range(ROWS):
                tb[n * 64:(n + 1) * 64, r * 128:(r + 1) * 128] = out[r * 64:(r + 1) * 64, n * 128:(n + 1) * 128]
        return chip * 2 + h

    def partial_copy(t, g):
        yy, xx = g * nc + y * c, x * nc + g * c
        return pltpu.make_async_remote_copy(
            src_ref=sb.at[t, g], dst_ref=r2.at[t, across], send_sem=send2.at[t],
            recv_sem=recv2.at[t], device_id=(z, dev(yy, xx, c)), device_id_type=MESH,
        )

    groups = [(across + j) % 4 for j in (2, 1, 3)]

    def send_partials(t):
        for g in groups:
            partial_copy(t, g).start()

    for p in range(PASSES):
        acc[p] = jnp.zeros(acc.shape[1:], F32)

        def step(i, carry):
            at = gather(p, i)
            for n in range(WIDE // 256):
                cols = slice(n * 256, (n + 1) * 256)
                acc[p, :, cols] = acc[p, :, cols] + mm(ph[at], tb[:, cols])
            return carry

        lax.fori_loop(0, 7, step, 0)
        at = gather(p, 7)
        for t in range(p * PER, (p + 1) * PER):
            for n in range(SUB // 256):
                here = slice(n * 256, (n + 1) * 256)
                start = (t % PER) * SUB + n * 256
                cols = slice(start, start + 256)
                full = acc[p, :, cols] + mm(ph[at], tb[:, cols])
                acc[p, :, cols] = full
                sb[t, :, :, here] = full.reshape(4, 256, 256).astype(BF16)
            send_partials(t)

    def owner_copy(t, o, zz, aa, cc):
        yy, xx = y * nc + aa * c, aa * nc + x * c
        return pltpu.make_async_remote_copy(
            src_ref=s3.at[t, o], dst_ref=r3.at[t, my_slot], send_sem=send3.at[t],
            recv_sem=recv3.at[t], device_id=(zz, dev(yy, xx, cc)), device_id_type=MESH,
        )

    me_o = z * 8 + along * 2 + c
    my_slot = z * 8 + c * 4 + along

    def finish(t, b):
        rows = pl.ds(pl.multiple_of(across * 256 + b * 64, 64), 64)
        part = pl.ds(pl.multiple_of(b * 64, 64), 64)
        n = t % PER
        total = acc[t // PER, rows, n * SUB:(n + 1) * SUB]
        for g in groups:
            total = total + r2[t, g, part, :].astype(F32)
        s3[t, pl.ds(b * 8, 8)] = total.reshape(8, 8, SUB).astype(BF16)

    def send_block(t, b):
        for i in range(8):
            aa, cc = i // 2, i % 2
            o = b * 8 + i

            @pl.when(o != me_o)
            def _():
                owner_copy(t, o, b, aa, cc).start()

    def collect(t):
        bytes_of(r3.at[t], recv3.at[t])

        def one(slot, carry):
            op, tile = slot // 16, slot % 16
            for r in range(SUB // 128):
                fs[pl.ds(op * 1024 + tile * 8 + (SUB // 128) * t + r, 8, stride=128), :] = r3[
                    t, slot, :, r * 128:(r + 1) * 128
                ].astype(F32)
            return carry

        lax.fori_loop(0, 32, one, 0)

    blocks = [(z + j) % 4 for j in (2, 1, 3, 0)]
    for t in range(SUBS):
        bytes_of(r2.at[t, pl.ds(0, 3)], recv2.at[t])
        for n, b in enumerate(blocks):
            finish(t, b)
            if n > 0:
                send_block(t, blocks[n - 1])
        send_block(t, blocks[3])
        pltpu.make_async_copy(s3.at[t, me_o], r3.at[t, my_slot], recv3.at[t]).start()
        if t >= LAG:
            collect(t - LAG)

    bytes_of(rc.at[pl.ds(0, 7)], c_send)
    bytes_of(rg.at[pl.ds(0, 7)], g_send)
    bytes_of(rd.at[:, pl.ds(0, 7), pl.ds(0, NR_LOC)], d_send)
    for t in range(SUBS):
        bytes_of(sb.at[t, pl.ds(0, 3)], send2.at[t])

    for t in range(max(SUBS - LAG, 0), SUBS):
        collect(t)

    v_copy.wait()
    for k2 in range(2):
        vs = vs_ref[k2].reshape(128, 128)
        sums = []
        for j in range(4):
            for ri in range(2):
                at = ((j // 2) * 8 + k2 * 4 + (j % 2) * 2 + ri) * 128
                sums.append(fs[at:at + 128, :].astype(BF16))
        left = mm(vs, jnp.concatenate(sums, axis=1))
        parts = []
        for j in range(4):
            lr = left[:, (2 * j) * 128:(2 * j + 1) * 128]
            li = left[:, (2 * j + 1) * 128:(2 * j + 2) * 128]
            parts.append(lr[:64] + li[64:])
            parts.append(li[:64] - lr[64:])
        stack = jnp.concatenate(parts, axis=0)
        high = stack.astype(BF16)
        low = (stack - high.astype(F32)).astype(BF16)
        vr, vi = vs_ref[k2, 0], vs_ref[k2, 1]
        yr = nt(high, vr) + nt(low, vr)
        yi = nt(high, vi) + nt(low, vi)
        res = []
        for j in range(4):
            a, b = slice(128 * j, 128 * j + 64), slice(128 * j + 64, 128 * j + 128)
            res.append((yr[a] - yi[b], yi[a] + yr[b]))
        (hr, hi), (dr, di), (ar, ai), (er, ei) = res
        qr, qi = hr - di, hi + dr
        pr, pi = hr + di, hi - dr

        def beside(*blocks):
            return jnp.concatenate(blocks, axis=1)

        first = jnp.concatenate([beside(ar, ai), beside(pr, pi)], axis=1)
        second = jnp.concatenate([beside(qr, qi), beside(-qi, qr), beside(ar, ai), beside(-ai, ar)], axis=0)
        f_high, s_high = first.astype(BF16), second.astype(BF16)
        f_low = (first - f_high.astype(F32)).astype(BF16)
        s_low = (second - s_high.astype(F32)).astype(BF16)
        both = mm(jnp.concatenate([f_high, f_low], axis=0), s_high)
        g[k2] = beside(er, ei) + FACTOR * (both[:64] + both[64:] + mm(f_high, s_low))
        even, odd = g[k2, pl.ds(0, 32, stride=2), :], g[k2, pl.ds(1, 32, stride=2), :]
        og[k2, 0] = beside(even[:, :64], odd[:, :64])
        og[k2, 1] = beside(even[:, 64:], odd[:, 64:])
        pltpu.make_async_copy(og.at[k2], out_ref.at[k2], l_sem.at[0]).start()

    for t in range(SUBS):
        bytes_of(s3.at[t, pl.ds(0, 31)], send3.at[t])
    bytes_of(og, l_sem.at[0])


def on_device(wannier_ops, r_coords, degeneracy, kpoints, bloch_vectors):
    ops = wannier_ops.reshape(2, NR_LOC, 2, 16, PASSES, ROWS, 128)
    dma = pltpu.SemaphoreType.DMA
    vmem = pltpu.VMEM
    res = pl.pallas_call(
        kernel,
        out_shape=jax.ShapeDtypeStruct((2, 2, 32, 128), F32),
        in_specs=[pl.BlockSpec(memory_space=pl.ANY)] * 5,
        out_specs=pl.BlockSpec(memory_space=pl.ANY),
        scratch_shapes=[
            vmem((8, 3, NR_LOC), I32),
            vmem((8, 1, NR_LOC), I32),
            vmem((PASSES, 8, 128, 2, ROWS, 128), BF16),
            vmem((3, 256), I32),
            vmem((2, 2, 64, 128), BF16),
            vmem((TALL, TALL), BF16),
            vmem((256, 256), BF16),
            vmem((128, 256), F32),
            vmem((256, 128), BF16),
            vmem((32, 256), F32),
            vmem((32, 256), F32),
            vmem((128, 128), BF16),
            vmem((2, 1024, 128), F32),
            vmem((8, 1024, 256), BF16),
            vmem((256, WIDE), BF16),
            vmem((PASSES, 1024, WIDE), F32),
            vmem((SUBS, 4, 256, SUB), BF16),
            vmem((SUBS, 4, 256, SUB), BF16),
            vmem((SUBS, 32, 8, SUB), BF16),
            vmem((SUBS, 32, 8, SUB), BF16),
            vmem((2048, 128), F32),
            vmem((2, 64, 128), F32),
            vmem((2, 2, 32, 128), F32),
            dma, dma, dma, dma, dma, dma((4, PASSES, 2)), dma((2,)),
            dma((SUBS,)), dma((SUBS,)), dma((SUBS,)), dma((SUBS,)),
        ],
        compiler_params=pltpu.CompilerParams(
            collective_id=0, has_side_effects=True, vmem_limit_bytes=54 * 1024 * 1024
        ),
    )(r_coords.T, degeneracy.reshape(1, NR_LOC), kpoints.T, bloch_vectors, ops)
    return res.reshape(2, 2, 4096)


def solution(mesh):
    in_specs = (
        P(None, "row", None, None, None),
        P("row", None),
        P("row"),
        P(),
        P(("op", "row"), None, None, None),
    )
    return jax.shard_map(
        on_device, mesh=mesh, in_specs=in_specs, out_specs=P(("op", "row"), None, None), check_vma=False
    )
```

time: 57.5 us -> 55 us (0.957)
  Pallas kernels: 55.7 us -> 53.4 us
    pallas_call x1, Pallas kernels: 55.7 us -> 53.4 us  [on_device(): pl.pallas_call(kernel, out_shape=jax.ShapeDtypeStruct((2, 2, 32, 128), F3...]
where the time goes in v3:
time: 55 us; the launch traced here: 54.9 us
  Pallas kernels  53.4 us (97%)
  local copies, waits for them, and re-layouts  1.5 us (3%)
    pallas_call x1, Pallas kernels, on_device(): pl.pallas_call(kernel, out_shape=jax.ShapeDtypeStruct((2, 2, 32, 128), F3...  53.4 us
    reshape x1, local copies, waits for them, and re-layouts, on_device(): return res.reshape(2, 2, 4096)  1.5 us

profile of v3, /device:TPU:1, one launch (start us, length us, event | category | flops | bytes accessed | tf_op | source)
XLA Modules:
  0.0 54.9 jit_solution(2359733283689849585)
XLA Ops:
  0.0 53.4 %shard_map.55 = f32[2,2,32,128]{3,2,1,0:T(8,128)} custom-call(s32[3,125]{1,0:T(4,128)} %bitcast.8, s32[1,125]{1,0:T(1,128)} %bitcast.9, s32[3,256]{1,0:T(4,128)} %bitcast.7, bf16[2,2,64,128]{3,2,1,0:T(8,128)(2,1)} %v_ref.1, bf16[2,125,2,16,4,2,128]{6,5,4,3,2,1,0:T(2,128)(2,1)} %bitcast.6), custom_call_target="tpu_custom_call" | custom-call | tf_op jit(solution)/shard_map/pallas_call | solution.py:371
  53.4 1.5 %reshape.11 = f32[2,2,4096]{2,1,0:T(2,128)} reshape(f32[2,2,32,128]{3,2,1,0:T(8,128)} %shard_map.55) | data formatting | bytes 131072 | tf_op jit(solution)/shard_map/reshape | solution.py:407

commit v4 on v3

--- a/solution.py
+++ b/solution.py
@@ -284,15 +284,12 @@
     def collect(t):
         bytes_of(r3.at[t], recv3.at[t])
 
-        def one(slot, carry):
+        for slot in range(32):
             op, tile = slot // 16, slot % 16
             for r in range(SUB // 128):
                 fs[pl.ds(op * 1024 + tile * 8 + (SUB // 128) * t + r, 8, stride=128), :] = r3[
                     t, slot, :, r * 128:(r + 1) * 128
                 ].astype(F32)
-            return carry
-
-        lax.fori_loop(0, 32, one, 0)
 
     blocks = [(z + j) % 4 for j in (2, 1, 3, 0)]
     for t in range(SUBS):
@@ -316,47 +313,49 @@
         collect(t)
 
     v_copy.wait()
+    def beside(*blocks):
+        return jnp.concatenate(blocks, axis=1)
+
+    def split(value):
+        high = value.astype(BF16)
+        return high, (value - high.astype(F32)).astype(BF16)
+
+    lefts, stacks, fields = [], [], []
     for k2 in range(2):
-        vs = vs_ref[k2].reshape(128, 128)
         sums = []
         for j in range(4):
             for ri in range(2):
                 at = ((j // 2) * 8 + k2 * 4 + (j % 2) * 2 + ri) * 128
                 sums.append(fs[at:at + 128, :].astype(BF16))
-        left = mm(vs, jnp.concatenate(sums, axis=1))
+        lefts.append(mm(vs_ref[k2].reshape(128, 128), beside(*sums)))
+    for left in lefts:
         parts = []
         for j in range(4):
             lr = left[:, (2 * j) * 128:(2 * j + 1) * 128]
             li = left[:, (2 * j + 1) * 128:(2 * j + 2) * 128]
             parts.append(lr[:64] + li[64:])
             parts.append(li[:64] - lr[64:])
-        stack = jnp.concatenate(parts, axis=0)
-        high = stack.astype(BF16)
-        low = (stack - high.astype(F32)).astype(BF16)
-        vr, vi = vs_ref[k2, 0], vs_ref[k2, 1]
-        yr = nt(high, vr) + nt(low, vr)
-        yi = nt(high, vi) + nt(low, vi)
+        stacks.append(jnp.concatenate(split(jnp.concatenate(parts, axis=0)), axis=0))
+    for k2, stack in enumerate(stacks):
+        yr, yi = nt(stack, vs_ref[k2, 0]), nt(stack, vs_ref[k2, 1])
+        yr, yi = yr[:512] + yr[512:], yi[:512] + yi[512:]
         res = []
         for j in range(4):
             a, b = slice(128 * j, 128 * j + 64), slice(128 * j + 64, 128 * j + 128)
             res.append((yr[a] - yi[b], yi[a] + yr[b]))
-        (hr, hi), (dr, di), (ar, ai), (er, ei) = res
+        fields.append(res)
+    for k2, ((hr, hi), (dr, di), (ar, ai), (er, ei)) in enumerate(fields):
         qr, qi = hr - di, hi + dr
         pr, pi = hr + di, hi - dr
-
-        def beside(*blocks):
-            return jnp.concatenate(blocks, axis=1)
-
-        first = jnp.concatenate([beside(ar, ai), beside(pr, pi)], axis=1)
+        first = beside(ar, ai, pr, pi)
         second = jnp.concatenate([beside(qr, qi), beside(-qi, qr), beside(ar, ai), beside(-ai, ar)], axis=0)
-        f_high, s_high = first.astype(BF16), second.astype(BF16)
-        f_low = (first - f_high.astype(F32)).astype(BF16)
-        s_low = (second - s_high.astype(F32)).astype(BF16)
+        (f_high, f_low), (s_high, s_low) = split(first), split(second)
         both = mm(jnp.concatenate([f_high, f_low], axis=0), s_high)
         g[k2] = beside(er, ei) + FACTOR * (both[:64] + both[64:] + mm(f_high, s_low))
+    for k2 in range(2):
         even, odd = g[k2, pl.ds(0, 32, stride=2), :], g[k2, pl.ds(1, 32, stride=2), :]
-        og[k2, 0] = beside(even[:, :64], odd[:, :64])
-        og[k2, 1] = beside(even[:, 64:], odd[:, 64:])
+        og[k2, pl.ds(0, 32, stride=2), :] = beside(even[:, :64], odd[:, :64])
+        og[k2, pl.ds(1, 32, stride=2), :] = beside(even[:, 64:], odd[:, 64:])
         pltpu.make_async_copy(og.at[k2], out_ref.at[k2], l_sem.at[0]).start()
 
     for t in range(SUBS):
@@ -370,7 +369,7 @@
     vmem = pltpu.VMEM
     res = pl.pallas_call(
         kernel,
-        out_shape=jax.ShapeDtypeStruct((2, 2, 32, 128), F32),
+        out_shape=jax.ShapeDtypeStruct((2, 64, 128), F32),
         in_specs=[pl.BlockSpec(memory_space=pl.ANY)] * 5,
         out_specs=pl.BlockSpec(memory_space=pl.ANY),
         scratch_shapes=[
@@ -396,7 +395,7 @@
             vmem((SUBS, 32, 8, SUB), BF16),
             vmem((2048, 128), F32),
             vmem((2, 64, 128), F32),
-            vmem((2, 2, 32, 128), F32),
+            vmem((2, 64, 128), F32),
             dma, dma, dma, dma, dma, dma((4, PASSES, 2)), dma((2,)),
             dma((SUBS,)), dma((SUBS,)), dma((SUBS,)), dma((SUBS,)),
         ],
@@ -404,7 +403,7 @@
             collective_id=0, has_side_effects=True, vmem_limit_bytes=54 * 1024 * 1024
         ),
     )(r_coords.T, degeneracy.reshape(1, NR_LOC), kpoints.T, bloch_vectors, ops)
-    return res.reshape(2, 2, 4096)
+    return jnp.swapaxes(res.reshape(2, 32, 2, 128), 1, 2).reshape(2, 2, 4096)
 
 
 def solution(mesh):

time: 55 us -> 54.1 us (0.984)
  Pallas kernels: 53.4 us -> 52.5 us
    reshape x1 -> x0, local copies, waits for them, and re-layouts: 1.5 us -> none  [on_device(): return res.reshape(2, 2, 4096)]
    unnamed x0 -> x1, local copies, waits for them, and re-layouts: none -> 1.47 us
    pallas_call x1, Pallas kernels: 53.4 us -> 52.5 us  [on_device(): pl.pallas_call(kernel, out_shape=jax.ShapeDtypeStruct((2, 64, 128), F32),...]
where the time goes in v4:
time: 54.1 us; the launch traced here: 54 us
  Pallas kernels  52.5 us (97%)
  local copies, waits for them, and re-layouts  1.47 us (3%)
    pallas_call x1, Pallas kernels, on_device(): pl.pallas_call(kernel, out_shape=jax.ShapeDtypeStruct((2, 64, 128), F32),...  52.5 us
    unnamed x1, local copies, waits for them, and re-layouts  1.47 us

profile of v4, /device:TPU:1, one launch (start us, length us, event | category | flops | bytes accessed | tf_op | source)
XLA Modules:
  0.0 54.0 jit_solution(4227832936066783584)
XLA Ops:
  0.0 52.5 %shard_map.55 = f32[2,64,128]{2,1,0:T(8,128)} custom-call(s32[3,125]{1,0:T(4,128)} %bitcast.12, s32[1,125]{1,0:T(1,128)} %bitcast.13, s32[3,256]{1,0:T(4,128)} %bitcast.11, bf16[2,2,64,128]{3,2,1,0:T(8,128)(2,1)} %v_ref.1, bf16[2,125,2,16,4,2,128]{6,5,4,3,2,1,0:T(2,128)(2,1)} %bitcast.9), custom_call_target="tpu_custom_call" | custom-call | tf_op jit(solution)/shard_map/pallas_call | solution.py:370
  52.5 1.5 %copy.8 = f32[2,2,4096]{2,1,0:T(2,128)} copy(f32[2,2,4096]{2,1,0:T(2,128)} %bitcast.10) | data formatting | bytes 131072

commit v5 on v4

--- a/solution.py
+++ b/solution.py
@@ -21,6 +21,7 @@
 PER = WIDE // SUB
 SUBS = PASSES * PER
 LAG = 2 if SUBS > 2 else 1
+VIA = 2
 TALL = 64 * ROWS
 FACTOR = 1.0 / 8.0
 S0 = 0.392698743691337 * 16.0
@@ -45,8 +46,8 @@
 
 
 def kernel(coord_ref, deg_ref, kp_ref, v_ref, ops_ref, out_ref, rc, rg, rd, kps, vs_ref, perm, pick,
-           kpp, kq, cm, wx, rmat, tw, ph, tb, acc, sb, r2, s3, r3, fs, g, og, c_send, c_recv, g_send, g_recv,
-           d_send, d_recv, l_sem, send2, recv2, send3, recv3):
+           kpp, kq, cm, wx, rmat, tw, ph, tb, acc, sb, r2, s3, r3, fs, g, og, far_in, far_out, c_send, c_recv, g_send, g_recv,
+           d_send, d_recv, l_sem, send2, recv2, send3, recv3, send_f, recv_f, send_v):
     z = lax.axis_index("op")
     row = lax.axis_index("row")
     y, x, c = row // 8, (row // 2) % 4, row % 2
@@ -231,6 +232,38 @@
         for g in groups:
             partial_copy(t, g).start()
 
+    def beside_me(d):
+        return (across + 1 + 2 * d) % 4
+
+    def line_copy(src, dst, sems, t, place):
+        yy, xx = place * nc + y * c, x * nc + place * c
+        return pltpu.make_async_remote_copy(
+            src_ref=src, dst_ref=dst, send_sem=sems[0].at[t], recv_sem=sems[1].at[t],
+            device_id=(z, dev(yy, xx, c)), device_id_type=MESH,
+        )
+
+    far = (across + 2) % 4
+
+    def send_halves(t):
+        for d in range(2):
+            part = pl.ds(d * 128, 128)
+            line_copy(sb.at[t, far, part], far_in.at[t, d], (send_f, recv_f), t, beside_me(d)).start()
+        for d in range(2):
+            part = pl.ds(d * 128, 128)
+            near = beside_me(1 - d)
+            line_copy(sb.at[t, near, part], r2.at[t, 0, part], (send2, recv2), t, near).start()
+
+    def forward(t):
+        bytes_of(far_in.at[t], recv_f.at[t])
+        n = t % PER
+        for d in range(2):
+            rows = pl.ds(pl.multiple_of(beside_me(d) * 256 + d * 128, 128), 128)
+            both = acc[t // PER, rows, n * SUB:(n + 1) * SUB] + far_in[t, d].astype(F32)
+            far_out[t, d] = both.astype(BF16)
+        for d in range(2):
+            part = pl.ds(d * 128, 128)
+            line_copy(far_out.at[t, d], r2.at[t, 1, part], (send_v, recv2), t, beside_me(d)).start()
+
     for p in range(PASSES):
         acc[p] = jnp.zeros(acc.shape[1:], F32)
 
@@ -242,6 +275,8 @@
             return carry
 
         lax.fori_loop(0, 7, step, 0)
+        if p == PASSES - 1:
+            forward(0)
         at = gather(p, 7)
         for t in range(p * PER, (p + 1) * PER):
             for n in range(SUB // 256):
@@ -251,7 +286,13 @@
                 full = acc[p, :, cols] + mm(ph[at], tb[:, cols])
                 acc[p, :, cols] = full
                 sb[t, :, :, here] = full.reshape(4, 256, 256).astype(BF16)
-            send_partials(t)
+            if t < VIA:
+                send_halves(t)
+            elif t < SUBS - 1:
+                send_partials(t)
+
+    forward(1)
+    send_partials(SUBS - 1)
 
     def owner_copy(t, o, zz, aa, cc):
         yy, xx = y * nc + aa * c, aa * nc + x * c
@@ -268,7 +309,7 @@
         part = pl.ds(pl.multiple_of(b * 64, 64), 64)
         n = t % PER
         total = acc[t // PER, rows, n * SUB:(n + 1) * SUB]
-        for g in groups:
+        for g in (groups if t >= VIA else (0, 1)):
             total = total + r2[t, g, part, :].astype(F32)
         s3[t, pl.ds(b * 8, 8)] = total.reshape(8, 8, SUB).astype(BF16)
 
@@ -293,7 +334,7 @@
 
     blocks = [(z + j) % 4 for j in (2, 1, 3, 0)]
     for t in range(SUBS):
-        bytes_of(r2.at[t, pl.ds(0, 3)], recv2.at[t])
+        bytes_of(r2.at[t, pl.ds(0, 3 if t >= VIA else 2)], recv2.at[t])
         for n, b in enumerate(blocks):
             finish(t, b)
             if n > 0:
@@ -306,7 +347,11 @@
     bytes_of(rc.at[pl.ds(0, 7)], c_send)
     bytes_of(rg.at[pl.ds(0, 7)], g_send)
     bytes_of(rd.at[:, pl.ds(0, 7), pl.ds(0, NR_LOC)], d_send)
-    for t in range(SUBS):
+    for t in range(VIA):
+        bytes_of(far_in.at[t], send_f.at[t])
+        bytes_of(far_in.at[t], send2.at[t])
+        bytes_of(far_out.at[t], send_v.at[t])
+    for t in range(VIA, SUBS):
         bytes_of(sb.at[t, pl.ds(0, 3)], send2.at[t])
 
     for t in range(max(SUBS - LAG, 0), SUBS):
@@ -396,8 +441,10 @@
             vmem((2048, 128), F32),
             vmem((2, 64, 128), F32),
             vmem((2, 64, 128), F32),
+            vmem((VIA, 2, 128, SUB), BF16),
+            vmem((VIA, 2, 128, SUB), BF16),
             dma, dma, dma, dma, dma, dma((4, PASSES, 2)), dma((2,)),
-            dma((SUBS,)), dma((SUBS,)), dma((SUBS,)), dma((SUBS,)),
+            dma((SUBS,)), dma((SUBS,)), dma((SUBS,)), dma((SUBS,)), dma((VIA,)), dma((VIA,)), dma((VIA,)),
         ],
         compiler_params=pltpu.CompilerParams(
             collective_id=0, has_side_effects=True, vmem_limit_bytes=54 * 1024 * 1024

time: 54.1 us -> 52.7 us (0.974)
  Pallas kernels: 52.5 us -> 51 us
    pallas_call x1, Pallas kernels: 52.5 us -> 51 us  [on_device(): pl.pallas_call(kernel, out_shape=jax.ShapeDtypeStruct((2, 64, 128), F32),...]
where the time goes in v5:
time: 52.7 us; the launch traced here: 52.5 us
  Pallas kernels  51 us (97%)
  local copies, waits for them, and re-layouts  1.47 us (3%)
    pallas_call x1, Pallas kernels, on_device(): pl.pallas_call(kernel, out_shape=jax.ShapeDtypeStruct((2, 64, 128), F32),...  51 us
    unnamed x1, local copies, waits for them, and re-layouts  1.47 us

profile of v5, /device:TPU:1, one launch (start us, length us, event | category | flops | bytes accessed | tf_op | source)
XLA Modules:
  0.0 52.5 jit_solution(9221568894072839637)
XLA Ops:
  0.0 51.0 %shard_map.55 = f32[2,64,128]{2,1,0:T(8,128)} custom-call(s32[3,125]{1,0:T(4,128)} %bitcast.12, s32[1,125]{1,0:T(1,128)} %bitcast.13, s32[3,256]{1,0:T(4,128)} %bitcast.11, bf16[2,2,64,128]{3,2,1,0:T(8,128)(2,1)} %v_ref.1, bf16[2,125,2,16,4,2,128]{6,5,4,3,2,1,0:T(2,128)(2,1)} %bitcast.9), custom_call_target="tpu_custom_call" | custom-call | tf_op jit(solution)/shard_map/pallas_call | solution.py:415
  51.0 1.5 %copy.8 = f32[2,2,4096]{2,1,0:T(2,128)} copy(f32[2,2,4096]{2,1,0:T(2,128)} %bitcast.10) | data formatting | bytes 131072

commit v6 on v5

--- a/solution.py
+++ b/solution.py
@@ -20,7 +20,7 @@
 SUB = 256
 PER = WIDE // SUB
 SUBS = PASSES * PER
-LAG = 2 if SUBS > 2 else 1
+LAG = SUBS
 VIA = 2
 TALL = 64 * ROWS
 FACTOR = 1.0 / 8.0
@@ -63,10 +63,6 @@
     def bytes_of(ref, sem):
         pltpu.make_async_copy(ref, ref, sem).wait()
 
-    for p in range(PASSES):
-        for s in range(8):
-            rd[p, s, pl.ds(NR_LOC, 3)] = jnp.zeros((3, 2, ROWS, 128), BF16)
-
     barrier = pltpu.get_barrier_semaphore()
 
     def greet(zz, rr):
@@ -149,6 +145,10 @@
         for k, h in order:
             slot, tile, target = peers[k]
             data_copy(slot, tile, p, h, target).start()
+
+    for p in range(PASSES):
+        for s in range(8):
+            rd[p, s, pl.ds(NR_LOC, 3)] = jnp.zeros((3, 2, ROWS, 128), BF16)
 
     o_i, i_i = iota((256, 256), 0), iota((256, 256), 1)
     p_o, p_i = iota((TALL, TALL), 0), iota((TALL, TALL), 1)

time: 52.7 us -> 52 us (0.987)
  Pallas kernels: 51 us -> 50.3 us
    pallas_call x1, Pallas kernels: 51 us -> 50.3 us  [on_device(): pl.pallas_call(kernel, out_shape=jax.ShapeDtypeStruct((2, 64, 128), F32),...]
where the time goes in v6:
time: 52 us; the launch traced here: 51.8 us
  Pallas kernels  50.3 us (97%)
  local copies, waits for them, and re-layouts  1.47 us (3%)
    pallas_call x1, Pallas kernels, on_device(): pl.pallas_call(kernel, out_shape=jax.ShapeDtypeStruct((2, 64, 128), F32),...  50.3 us
    unnamed x1, local copies, waits for them, and re-layouts  1.47 us

profile of v6, /device:TPU:1, one launch (start us, length us, event | category | flops | bytes accessed | tf_op | source)
XLA Modules:
  0.0 51.8 jit_solution(12448488908126255817)
XLA Ops:
  0.0 50.3 %shard_map.55 = f32[2,64,128]{2,1,0:T(8,128)} custom-call(s32[3,125]{1,0:T(4,128)} %bitcast.12, s32[1,125]{1,0:T(1,128)} %bitcast.13, s32[3,256]{1,0:T(4,128)} %bitcast.11, bf16[2,2,64,128]{3,2,1,0:T(8,128)(2,1)} %v_ref.1, bf16[2,125,2,16,4,2,128]{6,5,4,3,2,1,0:T(2,128)(2,1)} %bitcast.9), custom_call_target="tpu_custom_call" | custom-call | tf_op jit(solution)/shard_map/pallas_call | solution.py:415
  50.3 1.5 %copy.8 = f32[2,2,4096]{2,1,0:T(2,128)} copy(f32[2,2,4096]{2,1,0:T(2,128)} %bitcast.10) | data formatting | bytes 131072

commit v7 on v6

--- a/solution.py
+++ b/solution.py
@@ -232,6 +232,17 @@
         for g in groups:
             partial_copy(t, g).start()
 
+    def send_last():
+        for half in range(2):
+            part = pl.ds(half * 128, 128)
+            for g in groups:
+                yy, xx = g * nc + y * c, x * nc + g * c
+                pltpu.make_async_remote_copy(
+                    src_ref=sb.at[SUBS - 1, g, part], dst_ref=r2.at[SUBS - 1, across, part],
+                    send_sem=send2.at[SUBS - 1], recv_sem=recv2.at[SUBS - 1 + half],
+                    device_id=(z, dev(yy, xx, c)), device_id_type=MESH,
+                ).start()
+
     def beside_me(d):
         return (across + 1 + 2 * d) % 4
 
@@ -292,7 +303,7 @@
                 send_partials(t)
 
     forward(1)
-    send_partials(SUBS - 1)
+    send_last()
 
     def owner_copy(t, o, zz, aa, cc):
         yy, xx = y * nc + aa * c, aa * nc + x * c
@@ -306,7 +317,7 @@
 
     def finish(t, b):
         rows = pl.ds(pl.multiple_of(across * 256 + b * 64, 64), 64)
-        part = pl.ds(pl.multiple_of(b * 64, 64), 64)
+        part = pl.ds(b * 64 if isinstance(b, int) else pl.multiple_of(b * 64, 64), 64)
         n = t % PER
         total = acc[t // PER, rows, n * SUB:(n + 1) * SUB]
         for g in (groups if t >= VIA else (0, 1)):
@@ -334,12 +345,20 @@
 
     blocks = [(z + j) % 4 for j in (2, 1, 3, 0)]
     for t in range(SUBS):
-        bytes_of(r2.at[t, pl.ds(0, 3 if t >= VIA else 2)], recv2.at[t])
-        for n, b in enumerate(blocks):
-            finish(t, b)
-            if n > 0:
-                send_block(t, blocks[n - 1])
-        send_block(t, blocks[3])
+        if t < SUBS - 1:
+            bytes_of(r2.at[t, pl.ds(0, 3 if t >= VIA else 2)], recv2.at[t])
+            for n, b in enumerate(blocks):
+                finish(t, b)
+                if n > 0:
+                    send_block(t, blocks[n - 1])
+            send_block(t, blocks[3])
+        else:
+            for half in range(2):
+                bytes_of(r2.at[t, pl.ds(0, 3), pl.ds(half * 128, 128)], recv2.at[t + half])
+                for b in (2 * half, 2 * half + 1):
+                    finish(t, b)
+                for b in (2 * half, 2 * half + 1):
+                    send_block(t, b)
         pltpu.make_async_copy(s3.at[t, me_o], r3.at[t, my_slot], recv3.at[t]).start()
         if t >= LAG:
             collect(t - LAG)
@@ -444,7 +463,7 @@
             vmem((VIA, 2, 128, SUB), BF16),
             vmem((VIA, 2, 128, SUB), BF16),
             dma, dma, dma, dma, dma, dma((4, PASSES, 2)), dma((2,)),
-            dma((SUBS,)), dma((SUBS,)), dma((SUBS,)), dma((SUBS,)), dma((VIA,)), dma((VIA,)), dma((VIA,)),
+            dma((SUBS,)), dma((SUBS + 1,)), dma((SUBS,)), dma((SUBS,)), dma((VIA,)), dma((VIA,)), dma((VIA,)),
         ],
         compiler_params=pltpu.CompilerParams(
             collective_id=0, has_side_effects=True, vmem_limit_bytes=54 * 1024 * 1024

time: 52 us -> 51.1 us (0.983)
  Pallas kernels: 50.3 us -> 49.5 us
    pallas_call x1, Pallas kernels: 50.3 us -> 49.5 us  [on_device(): pl.pallas_call(kernel, out_shape=jax.ShapeDtypeStruct((2, 64, 128), F32),...]
where the time goes in v7:
time: 51.1 us; the launch traced here: 51 us
  Pallas kernels  49.5 us (97%)
  local copies, waits for them, and re-layouts  1.47 us (3%)
    pallas_call x1, Pallas kernels, on_device(): pl.pallas_call(kernel, out_shape=jax.ShapeDtypeStruct((2, 64, 128), F32),...  49.5 us
    unnamed x1, local copies, waits for them, and re-layouts  1.47 us

profile of v7, /device:TPU:1, one launch (start us, length us, event | category | flops | bytes accessed | tf_op | source)
XLA Modules:
  0.0 51.0 jit_solution(8247656814043589361)
XLA Ops:
  0.0 49.5 %shard_map.55 = f32[2,64,128]{2,1,0:T(8,128)} custom-call(s32[3,125]{1,0:T(4,128)} %bitcast.12, s32[1,125]{1,0:T(1,128)} %bitcast.13, s32[3,256]{1,0:T(4,128)} %bitcast.11, bf16[2,2,64,128]{3,2,1,0:T(8,128)(2,1)} %v_ref.1, bf16[2,125,2,16,4,2,128]{6,5,4,3,2,1,0:T(2,128)(2,1)} %bitcast.9), custom_call_target="tpu_custom_call" | custom-call | tf_op jit(solution)/shard_map/pallas_call | solution.py:434
  49.5 1.5 %copy.8 = f32[2,2,4096]{2,1,0:T(2,128)} copy(f32[2,2,4096]{2,1,0:T(2,128)} %bitcast.10) | data formatting | bytes 131072

commit v8 on v7

--- a/solution.py
+++ b/solution.py
@@ -233,13 +233,13 @@
             partial_copy(t, g).start()
 
     def send_last():
-        for half in range(2):
-            part = pl.ds(half * 128, 128)
+        for quarter in range(4):
+            part = pl.ds(quarter * 64, 64)
             for g in groups:
                 yy, xx = g * nc + y * c, x * nc + g * c
                 pltpu.make_async_remote_copy(
                     src_ref=sb.at[SUBS - 1, g, part], dst_ref=r2.at[SUBS - 1, across, part],
-                    send_sem=send2.at[SUBS - 1], recv_sem=recv2.at[SUBS - 1 + half],
+                    send_sem=send2.at[SUBS - 1], recv_sem=recv2.at[SUBS - 1 + quarter],
                     device_id=(z, dev(yy, xx, c)), device_id_type=MESH,
                 ).start()
 
@@ -353,12 +353,10 @@
                     send_block(t, blocks[n - 1])
             send_block(t, blocks[3])
         else:
-            for half in range(2):
-                bytes_of(r2.at[t, pl.ds(0, 3), pl.ds(half * 128, 128)], recv2.at[t + half])
-                for b in (2 * half, 2 * half + 1):
-                    finish(t, b)
-                for b in (2 * half, 2 * half + 1):
-                    send_block(t, b)
+            for b in range(4):
+                bytes_of(r2.at[t, pl.ds(0, 3), pl.ds(b * 64, 64)], recv2.at[t + b])
+                finish(t, b)
+                send_block(t, b)
         pltpu.make_async_copy(s3.at[t, me_o], r3.at[t, my_slot], recv3.at[t]).start()
         if t >= LAG:
             collect(t - LAG)
@@ -463,7 +461,7 @@
             vmem((VIA, 2, 128, SUB), BF16),
             vmem((VIA, 2, 128, SUB), BF16),
             dma, dma, dma, dma, dma, dma((4, PASSES, 2)), dma((2,)),
-            dma((SUBS,)), dma((SUBS + 1,)), dma((SUBS,)), dma((SUBS,)), dma((VIA,)), dma((VIA,)), dma((VIA,)),
+            dma((SUBS,)), dma((SUBS + 3,)), dma((SUBS,)), dma((SUBS,)), dma((VIA,)), dma((VIA,)), dma((VIA,)),
         ],
         compiler_params=pltpu.CompilerParams(
             collective_id=0, has_side_effects=True, vmem_limit_bytes=54 * 1024 * 1024

time: 51.1 us -> 51.1 us (level)
  no operation moved by 1% of the time
where the time goes in v8:
time: 51.1 us; the launch traced here: 51 us
  Pallas kernels  49.5 us (97%)
  local copies, waits for them, and re-layouts  1.47 us (3%)
    pallas_call x1, Pallas kernels, on_device(): pl.pallas_call(kernel, out_shape=jax.ShapeDtypeStruct((2, 64, 128), F32),...  49.5 us
    unnamed x1, local copies, waits for them, and re-layouts  1.47 us

profile of v8, /device:TPU:1, one launch (start us, length us, event | category | flops | bytes accessed | tf_op | source)
XLA Modules:
  0.0 51.0 jit_solution(12533753873546865149)
XLA Ops:
  0.0 49.5 %shard_map.55 = f32[2,64,128]{2,1,0:T(8,128)} custom-call(s32[3,125]{1,0:T(4,128)} %bitcast.12, s32[1,125]{1,0:T(1,128)} %bitcast.13, s32[3,256]{1,0:T(4,128)} %bitcast.11, bf16[2,2,64,128]{3,2,1,0:T(8,128)(2,1)} %v_ref.1, bf16[2,125,2,16,4,2,128]{6,5,4,3,2,1,0:T(2,128)(2,1)} %bitcast.9), custom_call_target="tpu_custom_call" | custom-call | tf_op jit(solution)/shard_map/pallas_call | solution.py:432
  49.5 1.5 %copy.8 = f32[2,2,4096]{2,1,0:T(2,128)} copy(f32[2,2,4096]{2,1,0:T(2,128)} %bitcast.10) | data formatting | bytes 131072
